TPU v7x, 128 devices: a whole 4x4x4 slice. The times are simulated.
128 devices in a mesh: seq: 16 (over z, x), tp: 8 (over y, core).
Axes of the slice: x: 4, y: 4, z: 4, core: 2. Of those that a mesh axis runs over, the one named last changes fastest.
Arguments:
- tokens: bfloat16 [2048, 6144], P('seq', 'tp'), may hold values from -6 to 6
- router_weight: bfloat16 [6144, 8], P('tp'), may hold values from -0.15625 to 0.15625
- expert_ids: int32 [2048, 2], P('seq'), may hold values from 0 to 7, all different within a row; in each aligned block of 128 rows (0 to 127, 128 to 255, ...) at most 56 rows name the same one
- gate_weight: bfloat16 [16, 6144, 4096], P('seq', None, 'tp'), may hold values from -0.078125 to 0.078125
- up_weight: bfloat16 [16, 6144, 4096], P('seq', None, 'tp'), may hold values from -0.078125 to 0.078125
- down_weight: bfloat16 [16, 4096, 6144], P('seq', 'tp'), may hold values from -0.0625 to 0.0625
Outputs:
- mixed: bfloat16 [2048, 6144], P('seq', 'tp')
Inputs may be any that keep to these rules, and one draw needn't show every extreme that they name: `expert_ids`: each row names 2 different experts. In each aligned block of 128 rows (the tokens of one sequence group) no expert is named more than 56 times, a bound that some block reaches.
All inputs are finite; a program needn't handle non-finite values.
Results may differ from a plain program's by a relative error of at most 0.014.
Values may be sent and summed in bfloat16 or wider, within the bound.
No kernel may reach another device: no remote copies, remote signals or barrier semaphores. Data moves between devices by JAX's collectives and lax.ppermute only.
A program may use at most 128 MiB of HBM per device.

v0:
```python
import jax
import jax.numpy as jnp
from jax import lax
from jax.sharding import PartitionSpec as P

D = 6144
CAP = 56


def sent_to_all(array, axis):
    length = lax.axis_size(axis)
    return lax.all_to_all(
        jnp.broadcast_to(array[None], (length, *array.shape)), axis, 0, 0, tiled=True
    )


def over_copies(array, axis):
    return sent_to_all(array, axis).sum(axis=0)


def slot_numbers(expert_ids, experts):
    flat_ids = expert_ids.reshape(-1)
    onehot = (flat_ids[:, None] == jnp.arange(experts, dtype=jnp.int32)[None, :]).astype(jnp.int32)
    before = jnp.cumsum(onehot, axis=0) - onehot
    return (flat_ids, jnp.sum(before * onehot, axis=1))


def per_device(tokens, router_weight, expert_ids, gate_weight, up_weight, down_weight):
    seq_count = lax.axis_size("seq")
    experts = router_weight.shape[1]
    halves = seq_count // experts
    tok_rows, top_count = expert_ids.shape
    capacity = CAP
    width = D
    gate_slab = gate_weight[0]
    up_slab = up_weight[0]
    down_slab = down_weight[0]
    partial_logits = jnp.dot(tokens, router_weight, preferred_element_type=jnp.float32)
    logits = over_copies(partial_logits, "tp")
    chosen = expert_ids[:, :, None] == jnp.arange(experts, dtype=jnp.int32)[None, None, :]
    picked = jnp.sum(jnp.where(chosen, logits[:, None, :], 0.0), axis=2)
    gates = jax.nn.sigmoid(picked - picked[:, ::-1])
    flat_ids, slots = slot_numbers(expert_ids, experts)
    row_index = jnp.arange(seq_count * capacity, dtype=jnp.int32)
    row_expert = row_index // capacity // halves
    row_slot = row_index % capacity
    matches = (row_expert[:, None] == flat_ids[None, :]) & (row_slot[:, None] == slots[None, :])
    select = jnp.any(matches.reshape(seq_count * capacity, tok_rows, top_count), axis=2).astype(
        jnp.bfloat16
    )
    outgoing = jnp.dot(select, tokens, preferred_element_type=jnp.float32).astype(jnp.bfloat16)
    outgoing = outgoing.reshape(seq_count, capacity, tokens.shape[1])
    received = lax.all_to_all(outgoing, "seq", split_axis=0, concat_axis=0, tiled=True)
    count = received.shape[1]
    piece = lax.all_gather(received, "tp", axis=2, tiled=True)
    piece_rows = piece.reshape(-1, piece.shape[2])
    gate = jnp.dot(piece_rows, gate_slab, preferred_element_type=jnp.float32)
    up = jnp.dot(piece_rows, up_slab, preferred_element_type=jnp.float32)
    hidden = (jax.nn.silu(gate) * up).astype(jnp.bfloat16)
    partial_value = jnp.dot(hidden, down_slab, preferred_element_type=jnp.float32).reshape(
        seq_count, count, width
    )
    reduced = lax.psum_scatter(
        partial_value.astype(jnp.bfloat16), "tp", scatter_dimension=2, tiled=True
    ).astype(jnp.float32)
    returned = lax.all_to_all(
        reduced.astype(jnp.bfloat16), "seq", split_axis=0, concat_axis=0, tiled=True
    ).astype(reduced.dtype)
    columns = returned.shape[2]
    summed = jnp.sum(returned.reshape(experts, halves, capacity, columns), axis=1)
    summed = summed.reshape(experts * capacity, columns)
    gathered = summed[flat_ids * capacity + slots].reshape(tok_rows, top_count, columns)
    mixed = jnp.sum(gathered * gates[:, :, None], axis=1)
    return mixed.astype(jnp.bfloat16)


def solution(mesh):
    in_specs = (
        P("seq", "tp"),
        P("tp", None),
        P("seq", None),
        P("seq", None, "tp"),
        P("seq", None, "tp"),
        P("seq", "tp", None),
    )
    out_specs = P("seq", "tp")
    return jax.shard_map(
        per_device, mesh=mesh, in_specs=in_specs, out_specs=out_specs, check_vma=False
    )
```

profile of v0, /device:TPU:9, one launch (start us, length us, event | category | flops | bytes accessed | tf_op | source)
XLA Modules:
  0.0 233.1 jit_solution(17153037409730043633)
XLA Ops:
  6.5 0.0 copy-start
  6.5 0.0 all-gather.2.cloned.1.call-start
  6.5 0.8 copy.27
  7.4 0.1 eq.78
  7.5 0.1 eq.74
  7.7 0.6 reduce-window.6
  8.3 0.2 slice_reduce_fusion
  8.5 0.1 fusion.8
  8.6 0.1 eq.82
  8.8 0.1 copy.29
  8.8 1.0 and_reduce_fusion
  9.9 0.0 copy-done
  9.9 0.5 convolution_convert_fusion.1
  10.4 27.4 %all_to_all.15 = bf16[16,56,768]{2,1,0:T(8,128)(2,1)} all-to-all(bf16[16,56,768]{2,1,0:T(8,128)(2,1)S(1)} %bitcast.37), channel_id=1, replica_groups=mesh['seq'=16,'tp'=8] {'seq'}, dimensions={0} | all-to-all | bytes 2752512 | tf_op jit(solution)/shard_map/all_to_all | solution.py:53
  37.8 0.0 all-gather.2.cloned.1.call-update
  37.8 0.0 reduce-scatter.2.cloned.1.call-start
  37.8 59.0 %all-gather.2.cloned.1.call-done = bf16[16,56,6144]{2,1,0:T(8,128)(2,1)} async-done(((bf16[16,56,768]{2,1,0:T(8,128)(2,1)}), bf16[16,56,6144]{2,1,0:T(8,128)(2,1)}) %all-gather.2.cloned.1.call-update) | async-done | bytes 11010064 | tf_op jit(solution)/shard_map/all_gather | solution.py:55
  96.9 0.0 copy-start.3
  96.9 10.6 %fusion.3 = f32[896,512]{1,0:T(8,128)S(1)} fusion(bf16[896,6144]{1,0:T(8,128)(2,1)} %bitcast.40, bf16[1,6144,512]{2,1,0:T(8,128)(2,1)} %param.9), kind=kOutput, calls=%fused_computation.5 | convolution fusion | flops 5637144576 | bytes 19136512 | tf_op jit(solution)/shard_map/dot_general | solution.py:57
  107.4 0.0 copy-done.3
  107.5 8.0 %multiply_convert_fusion = bf16[896,512]{1,0:T(8,128)(2,1)S(1)} fusion(f32[896,512]{1,0:T(8,128)S(1)} %fusion.3, bf16[896,6144]{1,0:T(8,128)(2,1)S(1)} %bitcast.41, bf16[1,6144,512]{2,1,0:T(8,128)(2,1)} %param.10), kind=kOutput, calls=%fused_computation.8 | convolution fusion | flops 5639897088 | bytes 20054016 | tf_op jit(solution)/shard_map/dot_general | solution.py:58
  115.5 11.3 %convolution_convert_fusion = bf16[16,56,6144]{2,1,0:T(8,128)(2,1)} fusion(bf16[16,56,512]{2,1,0:T(8,128)(2,1)S(1)} %bitcast.42, bf16[1,512,6144]{2,1,0:T(8,128)(2,1)} %param.11), kind=kOutput, calls=%fused_computation.1 | convolution fusion | flops 5642649600 | bytes 18219008 | tf_op jit(solution)/shard_map/dot_general | solution.py:60
  126.8 0.0 copy-start.2
  126.8 0.0 copy-start.1
  126.8 0.0 reduce-scatter.2.cloned.1.call-update
  126.9 0.7 copy-done.2
  127.5 0.1 fusion.19
  127.7 7.9 %all_to_all.16 = f32[8,128,8]{1,2,0:T(8,128)S(1)} all-to-all(f32[8,128,8]{1,2,0:T(8,128)S(1)} %broadcast_in_dim.10), channel_id=1, replica_groups=mesh['seq'=16,'tp'=8] {'tp'}, dimensions={0} | all-to-all | bytes 65536 | tf_op jit(solution)/shard_map/all_to_all | solution.py:12
  135.6 56.1 %reduce-scatter.2.cloned.1.call-done = bf16[16,56,768]{2,1,0:T(8,128)(2,1)} async-done(((bf16[16,56,6144]{2,1,0:T(8,128)(2,1)}), bf16[16,56,768]{2,1,0:T(8,128)(2,1)}) %reduce-scatter.2.cloned.1.call-update) | async-done | bytes 1376272 | tf_op jit(solution)/shard_map/reduce_scatter | solution.py:63
  191.7 6.7 %all-to-all-start.1 = ((bf16[16,56,768]{2,1,0:T(8,128)(2,1)}), bf16[16,56,768]{2,1,0:T(8,128)(2,1)S(1)}, u32[]{:S(2)}, u32[]{:S(2)}) async-start(bf16[16,56,768]{2,1,0:T(8,128)(2,1)} %reduce-scatter.2.cloned.1.call-done), calls=%async_computation.2 | async-start | bytes 2752512 | tf_op jit(solution)/shard_map/all_to_all | solution.py:66
  198.3 0.0 copy-done.1
  198.4 0.1 copy.30
  198.5 0.1 mul.39
  198.7 0.1 copy.31
  198.8 24.0 %all-to-all-done.1 = bf16[16,56,768]{2,1,0:T(8,128)(2,1)S(1)} async-done(((bf16[16,56,768]{2,1,0:T(8,128)(2,1)}), bf16[16,56,768]{2,1,0:T(8,128)(2,1)S(1)}, u32[]{:S(2)}, u32[]{:S(2)}) %all-to-all-start.1) | async-done | bytes 1376288 | tf_op jit(solution)/shard_map/all_to_all | solution.py:66
  222.8 0.2 convert_reduce_fusion
  223.0 1.1 gather_fusion
  224.1 0.5 reshape.133
  224.6 1.7 multiply_reduce_fusion
  (12 shorter events, 0.2 us)
Async XLA Ops:
  6.5 3.3 %copy-start = (bf16[128,768]{1,0:T(8,128)(2,1)S(1)}, bf16[128,768]{1,0:T(8,128)(2,1)}, u32[]{:S(2)}) copy-start(bf16[128,768]{1,0:T(8,128)(2,1)} %param.6) | copy-start | bytes 589828
  6.5 90.3 %all-gather.2.cloned.1.call-start = ((), (), s32[]{:S(2)}) async-start(), calls=%async_computation.4 | async-start | bytes 12386304 | tf_op jit(solution)/shard_map/all_gather | solution.py:55
  37.8 153.9 %reduce-scatter.2.cloned.1.call-start = ((), (), s32[]{:S(2)}) async-start(), calls=%async_computation.5 | async-start | bytes 12386304 | tf_op jit(solution)/shard_map/reduce_scatter | solution.py:63
  96.9 10.6 %copy-start.3 = (bf16[16,56,6144]{2,1,0:T(8,128)(2,1)S(1)}, bf16[16,56,6144]{2,1,0:T(8,128)(2,1)}, u32[]{:S(2)}) copy-start(bf16[16,56,6144]{2,1,0:T(8,128)(2,1)} %all-gather.2.cloned.1.call-done) | copy-start | bytes 33030148
  126.8 0.7 copy-start.2
  126.8 71.5 %copy-start.1 = (s32[128,2]{0,1:T(2,128)S(1)}, s32[128,2]{0,1:T(2,128)}, u32[]{:S(2)}) copy-start(s32[128,2]{0,1:T(2,128)} %param.8) | copy-start | bytes 3076
  191.7 31.1 %all-to-all-start.1 = ((bf16[16,56,768]{2,1,0:T(8,128)(2,1)}), bf16[16,56,768]{2,1,0:T(8,128)(2,1)S(1)}, u32[]{:S(2)}, u32[]{:S(2)}) async-start(bf16[16,56,768]{2,1,0:T(8,128)(2,1)} %reduce-scatter.2.cloned.1.call-done), calls=%async_computation.2 | async-start | bytes 2752512 | tf_op jit(solution)/shard_map/all_to_all | solution.py:66
Sparse Core Ops, SparseCore 0:
  37.9 58.9 all-gather.1
  127.0 64.6 reduce-scatter.1
where the time goes:
time: 233 us
  waiting for transfers between devices  139 us (60%)
  blocking collectives  35.3 us (15%)
  matrix products  30.6 us (13%)
  between operations  13.6 us (6%)
  starting transfers between devices  6.71 us (3%)
  local copies, waits for them, and re-layouts  4.17 us (2%)
  other arithmetic  3.74 us (2%)
    all_gather x1, waiting for transfers between devices, per_device(): piece = lax.all_gather(received, 'tp', axis=2, tiled=True)  59 us
    reduce_scatter x1, waiting for transfers between devices, per_device(): lax.psum_scatter(partial_value.astype(jnp.bfloat16), 'tp', scatter_dimens...  56.1 us
    all_to_all x1, blocking collectives, per_device(): lax.all_to_all(outgoing, 'seq', split_axis=0, concat_axis=0, tiled=True)  27.4 us
    all_to_all x1, waiting for transfers between devices, per_device(): lax.all_to_all(reduced.astype(jnp.bfloat16), 'seq', split_axis=0, concat_...  24 us
    dot_general x1, matrix products, per_device(): jnp.dot(hidden, down_slab, preferred_element_type=jnp.float32)  11.3 us
    dot_general x1, matrix products, per_device(): gate = jnp.dot(piece_rows, gate_slab, preferred_element_type=jnp.float32)  10.6 us
    dot_general x1, matrix products, per_device(): up = jnp.dot(piece_rows, up_slab, preferred_element_type=jnp.float32)  8.03 us
    all_to_all x1, blocking collectives, sent_to_all(): lax.all_to_all(jnp.broadcast_to(array[None], (length, *array.shape)), axi...  7.9 us
  transfers between devices with their start and end apart: 3, of which 3 were waited for; matrix products, arithmetic and copies ran while one was open for 0% of the time, Pallas kernels for 0%

commit v1 on v0

v1 whole, which is shorter than its diff:
```python
import jax
import jax.numpy as jnp
from jax import lax
from jax.experimental import pallas as pl
from jax.experimental.pallas import tpu as pltpu
from jax.sharding import PartitionSpec as P


D = 6144
CAP = 56
BLK = 768
NEAR = ((0, 0), (0, 1), (0, 3), (0, 2), (1, 0), (3, 0), (2, 0))
FAR = ((1, 1), (1, 2), (1, 3), (2, 1), (2, 2), (2, 3), (3, 1), (3, 2), (3, 3))
RELS = (0, 3, 1, 2)
VMEM_SPEC = pl.BlockSpec(memory_space=pltpu.VMEM)
ANY_SPEC = pl.BlockSpec(memory_space=pl.ANY)
SMEM_SPEC = pl.BlockSpec(memory_space=pltpu.SMEM)


def f32(array):
    return array.astype(jnp.float32)


def bf16(array):
    return array.astype(jnp.bfloat16)


def dot(a, b):
    return jnp.dot(a, b, preferred_element_type=jnp.float32)


def in_vmem(array):
    return pltpu.with_memory_space_constraint(array, pltpu.VMEM)


def seq_shift(array, shift):
    dz, dx = shift
    if shift == (0, 0):
        return array
    pairs = []
    for place in range(16):
        z, x = divmod(place, 4)
        pairs.append((place, (z + dz) % 4 * 4 + (x + dx) % 4))
    return lax.ppermute(array, "seq", pairs)


def y_shift(array, step):
    pairs = [(2 * y + c, 2 * ((y + step) % 4) + c) for y in range(4) for c in range(2)]
    return lax.ppermute(array, "tp", pairs)


def core_swap(array):
    return lax.ppermute(array, "tp", [(p, p ^ 1) for p in range(8)])


def block_start(where, index):
    other, rel = divmod(index, 4)
    return pl.multiple_of((2 * ((where[0] + rel) % 4) + (where[1] + other) % 2) * BLK, BLK)


def gate_body(pieces, count, started, where, refs):
    xs, (gate_w, up_w), rest = refs[:count], refs[count : count + 2], refs[count + 2 :]
    if started:
        gin, uin, gacc, uacc = rest
    else:
        gacc, uacc = rest
    seen = set()
    for block, operand, lane, start, size in pieces:
        cut = pl.ds(block_start(where, block), BLK)
        x = xs[operand][:, lane : lane + BLK]
        rows = pl.ds(start, size)
        gate, up = dot(x, gate_w[cut, :]), dot(x, up_w[cut, :])
        if start in seen:
            gacc[rows, :] += gate
            uacc[rows, :] += up
        elif started:
            gacc[rows, :] = gin[rows, :] + gate
            uacc[rows, :] = uin[rows, :] + up
        else:
            gacc[rows, :] = gate
            uacc[rows, :] = up
        seen.add(start)


def cost(rows, ffn, share):
    return pl.CostEstimate(
        flops=int(6 * rows * D * ffn * share), transcendentals=rows * ffn, bytes_accessed=6 * D * ffn
    )


def gate_part(where, xs, pieces, rows, gate_slab, up_slab):
    ffn = gate_slab.shape[1]
    count = len(xs)

    def body(where, *refs):
        gate_body(pieces, count, False, where, refs)

    out = jax.ShapeDtypeStruct((rows, ffn), jnp.float32)
    return pl.pallas_call(
        body,
        out_shape=(out, out),
        in_specs=[SMEM_SPEC] + [VMEM_SPEC] * (count + 2),
        out_specs=(VMEM_SPEC, VMEM_SPEC),
        compiler_params=pltpu.CompilerParams(vmem_limit_bytes=16 * 1024 * 1024),
        cost_estimate=cost(rows, ffn, 0.5),
    )(where, *[in_vmem(x) for x in xs], gate_slab, up_slab)


def down_blocks(where, hid, down_w, target, first, obuf, sem):
    stores = []
    for rel in range(4):
        obuf[first + rel] = bf16(dot(hid, down_w[:, pl.ds(block_start(where, first + rel), BLK)]))
        copy = pltpu.make_async_copy(obuf.at[first + rel], target.at[rel], sem.at[first + rel])
        copy.start()
        stores.append(copy)
    return stores


def expert(where, xs, pieces, rows, gate_slab, up_slab, down_slab, sums, whole):
    ffn = gate_slab.shape[1]
    count = len(xs)

    def body(where, *refs):
        xs_w, refs = refs[: count + 2], refs[count + 2 :]
        down_w, given, refs = refs[0], refs[1:3], refs[3:]
        if whole:
            send, keep, gacc, uacc, hid, obuf, sem = refs
        else:
            send, hid, gacc, uacc, obuf, sem = refs
        gate_body(pieces, count, True, where, (*xs_w, *given, gacc, uacc))
        gate = gacc[...]
        hid[...] = bf16(gate / (1.0 + jnp.exp(-gate)) * uacc[...])
        stores = down_blocks(where, hid[...], down_w, send, 4, obuf, sem)
        if whole:
            stores = stores + down_blocks(where, hid[...], down_w, keep, 0, obuf, sem)
        for copy in stores:
            copy.wait()

    out = jax.ShapeDtypeStruct((4, rows, BLK), jnp.bfloat16)
    hidden = jax.ShapeDtypeStruct((rows, ffn), jnp.bfloat16)
    scratch = [pltpu.VMEM((rows, ffn), jnp.float32), pltpu.VMEM((rows, ffn), jnp.float32)]
    if whole:
        scratch.append(pltpu.VMEM((rows, ffn), jnp.bfloat16))
    return pl.pallas_call(
        body,
        out_shape=(out, out if whole else hidden),
        in_specs=[SMEM_SPEC] + [VMEM_SPEC] * (count + 5),
        out_specs=(ANY_SPEC, ANY_SPEC if whole else VMEM_SPEC),
        scratch_shapes=[
            *scratch,
            pltpu.VMEM((8, rows, BLK), jnp.bfloat16),
            pltpu.SemaphoreType.DMA((8,)),
        ],
        compiler_params=pltpu.CompilerParams(vmem_limit_bytes=20 * 1024 * 1024),
        cost_estimate=cost(rows, ffn, 0.5),
    )(
        where,
        *[in_vmem(x) for x in xs],
        gate_slab,
        up_slab,
        down_slab,
        *[in_vmem(a) for a in sums],
    )


def down_part(where, hid, down_slab):
    rows, ffn = hid.shape

    def body(where, hid, down_w, keep, obuf, sem):
        for copy in down_blocks(where, hid[...], down_w, keep, 0, obuf, sem):
            copy.wait()

    return pl.pallas_call(
        body,
        out_shape=jax.ShapeDtypeStruct((4, rows, BLK), jnp.bfloat16),
        in_specs=[SMEM_SPEC, VMEM_SPEC, VMEM_SPEC],
        out_specs=ANY_SPEC,
        scratch_shapes=[
            pltpu.VMEM((4, rows, BLK), jnp.bfloat16),
            pltpu.SemaphoreType.DMA((4,)),
        ],
        compiler_params=pltpu.CompilerParams(vmem_limit_bytes=10 * 1024 * 1024),
        cost_estimate=cost(rows, ffn, 0.2),
    )(where, in_vmem(hid), down_slab)


def placed(places, sources, picks, length):
    shape = sources[0].shape[-2:]
    count = len(sources)

    def value(places, index):
        return places[-1 - index] if index < 0 else index

    def body(places, *refs):
        ins, out = refs[:count], refs[count]
        for source, index, target in picks:
            ref = ins[source]
            block = ref[value(places, index)] if len(ref.shape) == 3 else ref[...]
            out[value(places, target)] = block

    return pl.pallas_call(
        body,
        out_shape=jax.ShapeDtypeStruct((length, *shape), sources[0].dtype),
        in_specs=[SMEM_SPEC] + [VMEM_SPEC] * count,
        out_specs=VMEM_SPEC,
        compiler_params=pltpu.CompilerParams(vmem_limit_bytes=10 * 1024 * 1024),
    )(places, *[in_vmem(a) for a in sources])


def resident(arrays):
    count = len(arrays)

    def body(*refs):
        ins, outs, sem = refs[:count], refs[count : 2 * count], refs[2 * count]
        copies = [pltpu.make_async_copy(a, b, sem.at[i]) for i, (a, b) in enumerate(zip(ins, outs))]
        for copy in copies:
            copy.start()
        for copy in copies:
            copy.wait()

    return pl.pallas_call(
        body,
        out_shape=tuple(pltpu.VMEM(a.shape, a.dtype) for a in arrays),
        in_specs=[pl.BlockSpec(memory_space=pltpu.HBM)] * count,
        out_specs=(VMEM_SPEC,) * count,
        scratch_shapes=[pltpu.SemaphoreType.DMA((count,))],
        compiler_params=pltpu.CompilerParams(vmem_limit_bytes=1024 * 1024),
    )(*[pltpu.with_memory_space_constraint(a, pltpu.HBM) for a in arrays])


def far_back(homes, base, first, second, length):
    count, rows, width = base.shape

    def body(homes, base, first, second, out):
        for i in range(length):
            if i < count:
                out[homes[i]] = bf16(base[i] + f32(first[i]) + f32(second[i]))
            else:
                out[homes[i]] = jnp.zeros((rows, width), jnp.bfloat16)

    return pl.pallas_call(
        body,
        out_shape=jax.ShapeDtypeStruct((length, rows, width), jnp.bfloat16),
        in_specs=[SMEM_SPEC] + [VMEM_SPEC] * 3,
        out_specs=VMEM_SPEC,
        compiler_params=pltpu.CompilerParams(vmem_limit_bytes=12 * 1024 * 1024),
    )(homes, *[in_vmem(a) for a in (base, first, second)])


def last_sum(base, parts, high, low, values):
    count = len(parts)

    def body(base, high, low, values, *refs):
        total = base[...] + dot(high[...], values[...]) + dot(low[...], values[...])
        for part in refs[:count]:
            total = total + f32(part[...])
        refs[count][...] = bf16(total)

    return pl.pallas_call(
        body,
        out_shape=jax.ShapeDtypeStruct(base.shape, jnp.bfloat16),
        in_specs=[VMEM_SPEC] * (4 + count),
        out_specs=VMEM_SPEC,
        compiler_params=pltpu.CompilerParams(vmem_limit_bytes=12 * 1024 * 1024),
    )(base, high, low, values, *parts)


def near_mix(high, low, values):
    count = len(values)
    tok_rows = high.shape[1]
    over_slots = (((0,), (0,)), ((), ()))

    def body(high, low, *refs):
        ins, first, others = refs[:count], refs[count], refs[count + 1]
        for rel in range(4):
            total = jnp.zeros((tok_rows, BLK), jnp.float32)
            for i in range(count):
                part = ins[i][rel]
                for weights in (high, low):
                    total = total + lax.dot_general(
                        weights[i * CAP : (i + 1) * CAP, :],
                        part,
                        over_slots,
                        preferred_element_type=jnp.float32,
                    )
            if rel == 0:
                first[...] = total
            else:
                others[rel - 1] = bf16(total)

    return pl.pallas_call(
        body,
        out_shape=(
            jax.ShapeDtypeStruct((tok_rows, BLK), jnp.float32),
            jax.ShapeDtypeStruct((3, tok_rows, BLK), jnp.bfloat16),
        ),
        in_specs=[VMEM_SPEC] * (2 + count),
        out_specs=(VMEM_SPEC, VMEM_SPEC),
        compiler_params=pltpu.CompilerParams(vmem_limit_bytes=16 * 1024 * 1024),
    )(high, low, *values)


def layer(tokens, router_weight, expert_ids, gate_weight, up_weight, down_weight):
    experts = router_weight.shape[1]
    tok_rows, top_count = expert_ids.shape
    here = lax.axis_index("seq")
    tp = lax.axis_index("tp")
    where = jnp.stack([tp // 2, tp % 2]).astype(jnp.int32)
    slabs = resident([w[0] for w in (gate_weight, up_weight, down_weight)])
    slabs = tuple(in_vmem(w) for w in slabs)
    z_here, x_here = here // 4, here % 4

    def place(shift, sign=1):
        return (z_here + sign * shift[0]) % 4 * 4 + (x_here + sign * shift[1]) % 4

    logits = dot(tokens, router_weight)
    terms = []
    rest = logits
    for _ in range(3):
        term = lax.reduce_precision(rest, 8, 7)
        terms.append(bf16(term))
        rest = rest - term
    pad = jnp.zeros((tok_rows, 128 - 3 * experts), jnp.bfloat16)
    packed = jnp.concatenate([tokens, jnp.concatenate(terms + [pad], axis=1)], axis=1)
    gathered = [packed] + [y_shift(packed, step) for step in (1, 3, 2)]

    flat_ids = expert_ids.reshape(-1)
    total = tok_rows * top_count
    onehot = flat_ids[:, None] == jnp.arange(experts, dtype=jnp.int32)[None, :]
    earlier = (
        jnp.arange(total, dtype=jnp.int32)[:, None] > jnp.arange(total, dtype=jnp.int32)[None, :]
    )
    before = dot(bf16(earlier), bf16(onehot))
    slots = jnp.sum(jnp.where(onehot, before, 0.0), axis=1).astype(jnp.int32)
    token_keys = expert_ids * CAP + slots.reshape(tok_rows, top_count)

    all_keys = jnp.arange(16 * CAP, dtype=jnp.int32)
    all_keys = all_keys // (2 * CAP) * CAP + all_keys % CAP
    matches = jnp.any(all_keys[:, None, None] == token_keys[None], axis=2)
    out = bf16(dot(bf16(matches), tokens)).reshape(16, CAP, BLK)
    received = lax.all_to_all(out, "seq", 0, 0, tiled=True)
    sources = jnp.stack([place(k, -1) for k in FAR]).astype(jnp.int32)
    count = len(FAR)
    far_rows = count * CAP
    own = placed(sources, [received], [(0, -1 - i, i) for i in range(count)], count)
    own = own.reshape(far_rows, BLK)

    full = jnp.concatenate([a[:, :BLK] for a in gathered], axis=1)
    slot_index = jnp.arange(CAP, dtype=jnp.int32)
    near_keys = jnp.stack([place(k) // 2 for k in NEAR])[:, None] * CAP + slot_index[None, :]
    matches = jnp.any(near_keys.reshape(-1)[:, None, None] == token_keys[None], axis=2)
    out = bf16(dot(bf16(matches), full))
    near = [seq_shift(out[i * CAP : (i + 1) * CAP], k) for i, k in enumerate(NEAR)]
    near_rows = len(NEAR) * CAP
    near_in = placed(where, near, [(i, 0, i) for i in range(len(NEAR))], len(NEAR))
    near_in = near_in.reshape(near_rows, 4 * BLK)
    near_other = core_swap(near_in)

    half_sum = jnp.zeros((tok_rows, experts), jnp.float32)
    for a in gathered:
        for i in range(3):
            half_sum = half_sum + f32(a[:, BLK + i * experts : BLK + (i + 1) * experts])
    logits = half_sum + core_swap(half_sum)
    chosen = expert_ids[:, :, None] == jnp.arange(experts, dtype=jnp.int32)[None, None, :]
    picked = jnp.sum(jnp.where(chosen, logits[:, None, :], 0.0), axis=2)
    gates = jax.nn.sigmoid(picked - picked[:, ::-1])

    def weights_of(keys):
        hit = token_keys[:, :, None] == keys[None, None, :]
        weights = jnp.sum(jnp.where(hit, gates[:, :, None], 0.0), axis=1)
        high = bf16(weights)
        return high, bf16(weights - f32(high))

    pieces = [(rel, 0, lane * BLK, 0, near_rows) for lane, rel in enumerate(RELS)]
    sums = gate_part(where, [near_in], pieces, near_rows, *slabs[:2])
    pieces = [(4 + rel, 0, lane * BLK, 0, near_rows) for lane, rel in enumerate(RELS)]
    send, keep = expert(where, [near_other], pieces, near_rows, *slabs, sums, True)
    got = core_swap(send)
    summed = bf16(f32(keep) + f32(got))
    returned = []
    for i, (dz, dx) in enumerate(NEAR):
        returned.append(seq_shift(summed[:, i * CAP : (i + 1) * CAP], ((-dz) % 4, (-dx) % 4)))
    hit = near_keys.reshape(-1)[:, None, None] == token_keys.T[None]
    weights = jnp.sum(jnp.where(hit, gates.T[None], 0.0), axis=1)
    high = bf16(weights)
    low = bf16(weights - f32(high))
    total, parts = near_mix(high, low, returned)
    summands = [y_shift(parts[rel - 1], rel) for rel in (1, 3, 2)]

    cut = far_rows // 32 * 16
    up1, dn1 = y_shift(own, 1), y_shift(own, 3)
    up2, dn2 = y_shift(up1[:cut], 1), y_shift(dn1[cut:], 3)
    first = [own, up1, dn1]
    first = first + [core_swap(a) for a in first]
    pieces = []
    for i, rel in enumerate((0, 3, 1)):
        pieces.append((rel, i, 0, 0, far_rows))
        pieces.append((4 + rel, 3 + i, 0, 0, far_rows))
    sums = gate_part(where, first, pieces, far_rows, *slabs[:2])
    last = [up2, dn2]
    last = last + [core_swap(a) for a in last]
    pieces = []
    for other in range(2):
        pieces.append((4 * other + 2, 2 * other, 0, 0, cut))
        pieces.append((4 * other + 2, 2 * other + 1, 0, cut, far_rows - cut))
    send, hid = expert(where, last, pieces, far_rows, *slabs, sums, False)
    got = core_swap(send)
    keep = down_part(where, hid, slabs[2])
    across_sum = bf16(f32(keep[2]) + f32(got[2]))
    from_below = y_shift(across_sum[:cut], 1)
    from_above = y_shift(across_sum[cut:], 3)
    zero_low = jnp.zeros((far_rows - cut, BLK), jnp.float32)
    zero_high = jnp.zeros((cut, BLK), jnp.float32)
    to_above = f32(keep[1]) + f32(got[1]) + jnp.concatenate([f32(from_below), zero_low], axis=0)
    to_below = f32(keep[3]) + f32(got[3]) + jnp.concatenate([zero_high, f32(from_above)], axis=0)
    shape = (count, CAP, BLK)
    homes = jnp.stack([place(k, -1) for k in FAR + NEAR]).astype(jnp.int32)
    base = (f32(keep[0]) + f32(got[0])).reshape(shape)
    from_below = y_shift(bf16(to_above), 1).reshape(shape)
    from_above = y_shift(bf16(to_below), 3).reshape(shape)
    back = far_back(homes, base, from_below, from_above, 16)
    values = lax.all_to_all(back, "seq", 0, 0, tiled=True).reshape(16 * CAP, BLK)
    seat = jnp.arange(16 * CAP, dtype=jnp.int32) // CAP
    is_far = (seat // 4 != z_here) & (seat % 4 != x_here)
    high, low = weights_of(jnp.where(is_far, all_keys, -1))
    return last_sum(total, summands, high, low, values)


def solution(mesh):
    in_specs = (
        P("seq", "tp"),
        P("tp", None),
        P("seq", None),
        P("seq", None, "tp"),
        P("seq", None, "tp"),
        P("seq", "tp", None),
    )
    out_specs = P("seq", "tp")
    return jax.shard_map(layer, mesh=mesh, in_specs=in_specs, out_specs=out_specs, check_vma=False)
```

time: 233 us -> 218 us (0.936)
  the two profiles are of different devices: /device:TPU:9 before, /device:TPU:34 now
where the time goes in v1:
time: 218 us; the launch traced here: 217 us
  waiting for transfers between devices  90 us (41%)
  starting transfers between devices  56.1 us (26%)
  Pallas kernels  44 us (20%)
  local copies, waits for them, and re-layouts  12.5 us (6%)
  other arithmetic  8.85 us (4%)
  matrix products  5.06 us (2%)
    ppermute x12, waiting for transfers between devices, seq_shift(): return lax.ppermute(array, 'seq', pairs)  49.1 us
    ppermute x14, waiting for transfers between devices, y_shift(): return lax.ppermute(array, 'tp', pairs)  38.8 us
    ppermute x14, starting transfers between devices, y_shift(): return lax.ppermute(array, 'tp', pairs)  19.4 us
    ppermute x12, starting transfers between devices, seq_shift(): return lax.ppermute(array, 'seq', pairs)  15.7 us
    pallas_call x2, Pallas kernels, expert(): pl.pallas_call(body, out_shape=(out, out if whole else hidden), in_specs=...  14.2 us
    all_to_all x1, starting transfers between devices, layer(): lax.all_to_all(back, 'seq', 0, 0, tiled=True).reshape(16 * CAP, BLK)  10.9 us
    pallas_call x2, Pallas kernels, gate_part(): pl.pallas_call(body, out_shape=(out, out), in_specs=[SMEM_SPEC] + [VMEM_S...  10.4 us
    all_to_all x1, starting transfers between devices, layer(): received = lax.all_to_all(out, 'seq', 0, 0, tiled=True)  7.87 us
  transfers between devices with their start and end apart: 37, of which 19 were waited for; matrix products, arithmetic and copies ran while one was open for 8% of the time, Pallas kernels for 18%

profile of v1, /device:TPU:34, one launch (start us, length us, event | category | flops | bytes accessed | tf_op | source)
XLA Modules:
  0.0 217.0 jit_solution(17259357586575262957)
XLA Ops:
  2.3 2.5 %convolution_convert_fusion.1 = bf16[896,768]{1,0:T(8,128)(2,1)} fusion(pred[896,128]{1,0:T(8,128)(4,1)S(1)} %compare_reduce_fusion, bf16[128,768]{1,0:T(8,128)(2,1)} %param.6), kind=kOutput, calls=%fused_computation.2 | convolution fusion | flops 176848896 | bytes 1687552 | tf_op jit(solution)/shard_map/dot_general | solution.py:29
  4.8 7.9 %all-to-all-start = ((bf16[16,56,768]{2,1,0:T(8,128)(2,1)}), bf16[16,56,768]{2,1,0:T(8,128)(2,1)S(1)}, u32[]{:S(2)}, u32[]{:S(2)}) async-start(bf16[16,56,768]{2,1,0:T(8,128)(2,1)} %bitcast.31), calls=%async_computation | async-start | bytes 2752512 | tf_op jit(solution)/shard_map/all_to_all | solution.py:341
  13.1 3.3 %collective-permute-start.2 = (bf16[128,896]{0,1:T(8,128)(2,1)S(1)}, bf16[128,896]{0,1:T(8,128)(2,1)S(1)}, u32[]{:S(2)}, u32[]{:S(2)}) collective-permute-start(bf16[128,896]{0,1:T(8,128)(2,1)S(1)} %broadcast_dynamic-update-slice_fusion), channel_id=1, source_target_pairs={{0,4},{1,5},{2,6},{3,7},{4,0},{5,1},{6,2},{7,3},{8,12},{9,13},{10,... | collective-permute-start | bytes 688136 | tf_op jit(solution)/shard_map/ppermute | solution.py:49
  18.9 4.3 %collective-permute-done.2 = bf16[128,896]{0,1:T(8,128)(2,1)S(1)} collective-permute-done((bf16[128,896]{0,1:T(8,128)(2,1)S(1)}, bf16[128,896]{0,1:T(8,128)(2,1)S(1)}, u32[]{:S(2)}, u32[]{:S(2)}) %collective-permute-start.2) | collective-permute-done | bytes 229408 | tf_op jit(solution)/shard_map/ppermute | solution.py:49
  23.2 3.6 %collective-permute-done.1 = bf16[128,896]{0,1:T(8,128)(2,1)S(1)} collective-permute-done((bf16[128,896]{0,1:T(8,128)(2,1)S(1)}, bf16[128,896]{0,1:T(8,128)(2,1)S(1)}, u32[]{:S(2)}, u32[]{:S(2)}) %collective-permute-start.1) | collective-permute-done | bytes 229408 | tf_op jit(solution)/shard_map/ppermute | solution.py:49
  26.8 2.2 %convolution_convert_fusion = bf16[392,3072]{1,0:T(8,128)(2,1)} fusion(pred[392,128]{1,0:T(8,128)(4,1)S(1)} %compare_reduce_fusion.1, bf16[128,768]{0,1:T(8,128)(2,1)S(1)} %slice.183, bf16[128,768]{0,1:T(8,128)(2,1)S(1)} %slice.182, bf16[128,768]{0,1:T(8,128)(2,1)S(1)} %slice.181, bf16[128,768]{0,1:T(8,128)(2,1)S(1)} %copy.35), kind=kOutput, calls=%fused_computation.1 | convolution fusion | flops 312631296 | bytes 3245056 | tf_op jit(solution)/shard_map/dot_general | solution.py:29
  30.7 1.6 collective-permute-start.18
  32.4 1.7 collective-permute-start.20
  34.0 1.8 fusion.31
  35.8 2.2 collective-permute-start.4
  38.0 2.5 %collective-permute-start.6 = (bf16[56,3072]{1,0:T(8,128)(2,1)S(1)}, bf16[56,3072]{1,0:T(8,128)(2,1)S(1)}, u32[]{:S(2)}, u32[]{:S(2)}) collective-permute-start(bf16[56,3072]{1,0:T(8,128)(2,1)S(1)} %get-tuple-element.49), channel_id=1, source_target_pairs={{0,16},{8,24},{16,0},{24,8},{32,48},{40,56},{48,32},{56,40},{64,80... | collective-permute-start | bytes 1032200 | tf_op jit(solution)/shard_map/ppermute | solution.py:44
  40.5 12.0 %collective-permute-done.4.refs_1_ = bf16[56,3072]{1,0:T(8,128)(2,1)S(1)} collective-permute-done((bf16[56,3072]{1,0:T(8,128)(2,1)S(1)}, bf16[56,3072]{1,0:T(8,128)(2,1)S(1)}, u32[]{:S(2)}, u32[]{:S(2)}) %collective-permute-start.4) | collective-permute-done | bytes 344096 | tf_op jit(solution)/shard_map/ppermute | solution.py:44
  52.4 1.1 collective-permute-start.7
  55.6 5.5 %collective-permute-done.7.refs_4_ = bf16[56,3072]{1,0:T(8,128)(2,1)S(1)} collective-permute-done((bf16[56,3072]{1,0:T(8,128)(2,1)S(1)}, bf16[56,3072]{1,0:T(8,128)(2,1)S(1)}, u32[]{:S(2)}, u32[]{:S(2)}) %collective-permute-start.7) | collective-permute-done | bytes 344096 | tf_op jit(solution)/shard_map/ppermute | solution.py:44
  61.2 1.8 slice.199
  63.0 2.7 %collective-permute-done.8.refs_5_ = bf16[56,3072]{1,0:T(8,128)(2,1)S(1)} collective-permute-done((bf16[56,3072]{1,0:T(8,128)(2,1)S(1)}, bf16[56,3072]{1,0:T(8,128)(2,1)S(1)}, u32[]{:S(2)}, u32[]{:S(2)}) %collective-permute-start.8) | collective-permute-done | bytes 344096 | tf_op jit(solution)/shard_map/ppermute | solution.py:44
  66.4 1.7 collective-permute-start.21
  68.0 1.8 slice.198
  69.8 3.8 %collective-permute-done.9.refs_6_ = bf16[56,3072]{1,0:T(8,128)(2,1)S(1)} collective-permute-done((bf16[56,3072]{1,0:T(8,128)(2,1)S(1)}, bf16[56,3072]{1,0:T(8,128)(2,1)S(1)}, u32[]{:S(2)}, u32[]{:S(2)}) %collective-permute-start.9) | collective-permute-done | bytes 344096 | tf_op jit(solution)/shard_map/ppermute | solution.py:44
  74.5 6.5 %shard_map.65 = (bf16[6144,512]{1,0:T(8,128)(2,1)S(1)}, bf16[6144,512]{1,0:T(8,128)(2,1)S(1)}, bf16[512,6144]{1,0:T(8,128)(2,1)S(1)}) custom-call(bf16[6144,512]{1,0:T(8,128)(2,1)} %bitcast.69, bf16[6144,512]{1,0:T(8,128)(2,1)} %bitcast.70, bf16[512,6144]{1,0:T(8,128)(2,1)} %bitcast.71), custom_call_target="tpu_custom_call" | custom-call | tf_op jit(solution)/shard_map/pallas_call | solution.py:221
  81.9 3.9 %collective-permute-done.19.refs_0_ = bf16[240,768]{1,0:T(8,128)(2,1)S(1)} collective-permute-done((bf16[240,768]{1,0:T(8,128)(2,1)}, bf16[240,768]{1,0:T(8,128)(2,1)S(1)}, u32[]{:S(2)}, u32[]{:S(2)}) %collective-permute-start.19) | collective-permute-done | bytes 368672 | tf_op jit(solution)/shard_map/ppermute | solution.py:49
  86.3 7.1 %shard_map.70 = (f32[504,512]{1,0:T(8,128)S(1)}, f32[504,512]{1,0:T(8,128)S(1)}) custom-call(s32[2]{0:T(128)S(1)} %pad_add_fusion.places.where, bf16[504,768]{1,0:T(8,128)(2,1)S(1)} %bitcast.68, bf16[504,768]{1,0:T(8,128)(2,1)} %collective-permute-done.18.refs_1_, bf16[504,768]{1,0:T(8,128)(2,1)} %collective-permute-done.20.refs_2_, ...), custom_call_target="tpu_custom_call" | custom-call | flops 4756340736 | bytes 18874368 | tf_op jit(solution)/shard_map/pallas_call | solution.py:99
  93.4 6.7 %shard_map.71 = (bf16[4,504,768]{2,1,0:T(8,128)(2,1)S(1)}, bf16[504,512]{1,0:T(8,128)(2,1)S(1)}) custom-call(s32[2]{0:T(128)S(1)} %pad_add_fusion.places.where, bf16[240,768]{1,0:T(8,128)(2,1)S(1)} %collective-permute-done.19.refs_0_, bf16[264,768]{1,0:T(8,128)(2,1)S(1)} %collective-permute-done.21.refs_1_, ...), custom_call_target="tpu_custom_call" | custom-call | flops 4756340736 | bytes 18874368 | tf_op jit(solution)/shard_map/pallas_call | solution.py:144
  100.2 3.3 %shard_map.66 = (f32[392,512]{1,0:T(8,128)S(1)}, f32[392,512]{1,0:T(8,128)S(1)}) custom-call(s32[2]{0:T(128)S(1)} %pad_add_fusion.places.where, bf16[392,3072]{1,0:T(8,128)(2,1)S(1)} %bitcast.61, bf16[6144,512]{1,0:T(8,128)(2,1)S(1)} %get-tuple-element.18.refs_1_.refs_6_.refs_4_, bf16[6144,512]{1,0:T(8,128)(2,1)S(1)} %get-tuple-element.19.refs_2_.refs_7_.refs_5_), custom_call_target="tpu_custom_call" | custom-call | flops 3699376128 | bytes 18874368 | tf_op jit(solution)/shard_map/pallas_call | solution.py:99
  103.5 7.6 %shard_map.67 = (bf16[4,392,768]{2,1,0:T(8,128)(2,1)}, bf16[4,392,768]{2,1,0:T(8,128)(2,1)S(1)}) custom-call(s32[2]{0:T(128)S(1)} %pad_add_fusion.places.where, bf16[392,3072]{1,0:T(8,128)(2,1)S(1)} %collective-permute-done.10.refs_0_, bf16[6144,512]{1,0:T(8,128)(2,1)S(1)} %get-tuple-element.18.refs_1_.refs_6_.refs_4_, ...), custom_call_target="tpu_custom_call" | custom-call | flops 3699376128 | bytes 18874368 | tf_op jit(solution)/shard_map/pallas_call | solution.py:144
  111.8 4.8 %shard_map.72 = bf16[4,504,768]{2,1,0:T(8,128)(2,1)S(1)} custom-call(s32[2]{0:T(128)S(1)} %pad_add_fusion.places.where, bf16[504,512]{1,0:T(8,128)(2,1)S(1)} %get-tuple-element.28.hid, bf16[512,6144]{1,0:T(8,128)(2,1)S(1)} %get-tuple-element.20.refs_3_.refs_6_.down_w), custom_call_target="tpu_custom_call" | custom-call | flops 1902536320 | bytes 18874368 | tf_op jit(solution)/shard_map/pallas_call | solution.py:173
  117.6 1.7 collective-permute-start.28
  119.3 9.9 %collective-permute-done.28 = bf16[240,768]{1,0:T(8,128)(2,1)S(1)} collective-permute-done((bf16[240,768]{1,0:T(8,128)(2,1)S(1)}, bf16[240,768]{1,0:T(8,128)(2,1)S(1)}, u32[]{:S(2)}, u32[]{:S(2)}) %collective-permute-start.28) | collective-permute-done | bytes 368672 | tf_op jit(solution)/shard_map/ppermute | solution.py:49
  129.1 1.7 fusion
  131.2 2.9 %collective-permute-start.31 = (bf16[504,768]{1,0:T(8,128)(2,1)}, bf16[504,768]{1,0:T(8,128)(2,1)}, u32[]{:S(2)}, u32[]{:S(2)}) collective-permute-start(bf16[504,768]{1,0:T(8,128)(2,1)} %get-tuple-element.35), channel_id=1, source_target_pairs={{0,6},{1,7},{2,0},{3,1},{4,2},{5,3},{6,4},{7,5},{8,14},{9,15},{10,... | collective-permute-start | bytes 2322440 | tf_op jit(solution)/shard_map/ppermute | solution.py:49
  136.1 4.4 %add_convert_fusion = bf16[4,392,768]{2,1,0:T(8,128)(2,1)} fusion(bf16[4,392,768]{2,1,0:T(8,128)(2,1)} %collective-permute-done.11, bf16[4,392,768]{2,1,0:T(8,128)(2,1)} %copy-done.2), kind=kLoop, calls=%fused_computation | loop fusion | flops 4816896 | bytes 7225344 | tf_op jit(solution)/shard_map/convert_element_type | solution.py:25
  140.5 9.8 %collective-permute-done.29 = bf16[504,768]{1,0:T(8,128)(2,1)S(1)} collective-permute-done((bf16[504,768]{1,0:T(8,128)(2,1)}, bf16[504,768]{1,0:T(8,128)(2,1)S(1)}, u32[]{:S(2)}, u32[]{:S(2)}) %collective-permute-start.29) | collective-permute-done | bytes 774176 | tf_op jit(solution)/shard_map/ppermute | solution.py:49
  151.2 1.1 copy-done.4
  152.4 2.5 %shard_map.73 = bf16[16,56,768]{2,1,0:T(8,128)(2,1)} custom-call(s32[16]{0:T(128)S(1)} %stack.123.homes, f32[9,56,768]{2,1,0:T(8,128)S(1)} %bitcast.62, bf16[9,56,768]{2,1,0:T(8,128)(2,1)S(1)} %bitcast.64, bf16[9,56,768]{2,1,0:T(8,128)(2,1)} %bitcast.39.second), custom_call_target="tpu_custom_call" | custom-call | tf_op jit(solution)/shard_map/pallas_call | solution.py:241
  154.9 10.9 %all-to-all-start.1 = ((bf16[16,56,768]{2,1,0:T(8,128)(2,1)}), bf16[16,56,768]{2,1,0:T(8,128)(2,1)S(1)}, u32[]{:S(2)}, u32[]{:S(2)}) async-start(bf16[16,56,768]{2,1,0:T(8,128)(2,1)} %shard_map.73), calls=%async_computation.1 | async-start | bytes 2752512 | tf_op jit(solution)/shard_map/all_to_all | solution.py:422
  165.8 1.8 fusion.30
  168.4 1.5 collective-permute-start.13
  170.0 3.3 %collective-permute-start.14 = (bf16[4,56,768]{2,1,0:T(8,128)(2,1)S(1)}, bf16[4,56,768]{2,1,0:T(8,128)(2,1)S(1)}, u32[]{:S(2)}, u32[]{:S(2)}) collective-permute-start(bf16[4,56,768]{2,1,0:T(8,128)(2,1)S(1)} %get-tuple-element.42), channel_id=1, source_target_pairs={{0,16},{8,24},{16,0},{24,8},{32,48},{40,56},{48,32},{56,40},{64,80... | collective-permute-start | bytes 1032200 | tf_op jit(solution)/shard_map/ppermute | solution.py:44
  173.8 1.5 collective-permute-start.16
  175.3 16.1 %collective-permute-done.12.refs_1_ = bf16[4,56,768]{2,1,0:T(8,128)(2,1)S(1)} collective-permute-done((bf16[4,56,768]{2,1,0:T(8,128)(2,1)S(1)}, bf16[4,56,768]{2,1,0:T(8,128)(2,1)S(1)}, u32[]{:S(2)}, u32[]{:S(2)}) %collective-permute-start.12) | collective-permute-done | bytes 344096 | tf_op jit(solution)/shard_map/ppermute | solution.py:44
  191.4 2.1 collective-permute-start.17
  194.1 2.2 %collective-permute-done.14.refs_3_ = bf16[4,56,768]{2,1,0:T(8,128)(2,1)S(1)} collective-permute-done((bf16[4,56,768]{2,1,0:T(8,128)(2,1)S(1)}, bf16[4,56,768]{2,1,0:T(8,128)(2,1)S(1)}, u32[]{:S(2)}, u32[]{:S(2)}) %collective-permute-start.14) | collective-permute-done | bytes 344096 | tf_op jit(solution)/shard_map/ppermute | solution.py:44
  196.3 5.3 %collective-permute-done.17.refs_6_ = bf16[4,56,768]{2,1,0:T(8,128)(2,1)S(1)} collective-permute-done((bf16[4,56,768]{2,1,0:T(8,128)(2,1)S(1)}, bf16[4,56,768]{2,1,0:T(8,128)(2,1)S(1)}, u32[]{:S(2)}, u32[]{:S(2)}) %collective-permute-start.17) | collective-permute-done | bytes 344096 | tf_op jit(solution)/shard_map/ppermute | solution.py:44
  201.6 3.0 %shard_map.68 = (f32[128,768]{1,0:T(8,128)S(1)}, bf16[3,128,768]{2,1,0:T(8,128)(2,1)S(1)}) custom-call(bf16[392,128]{1,0:T(8,128)(2,1)S(1)} %get-tuple-element.34.high, bf16[392,128]{1,0:T(8,128)(2,1)S(1)} %get-tuple-element.33.low, bf16[4,56,768]{2,1,0:T(8,128)(2,1)S(1)} %get-tuple-element.45.refs_0_, ...), custom_call_target="tpu_custom_call" | custom-call | tf_op jit(solution)/shard_map/pallas_call | solution.py:291
  204.7 3.2 %collective-permute-start.33 = (bf16[128,768]{1,0:T(8,128)(2,1)S(1)}, bf16[128,768]{1,0:T(8,128)(2,1)S(1)}, u32[]{:S(2)}, u32[]{:S(2)}) collective-permute-start(bf16[128,768]{1,0:T(8,128)(2,1)S(1)} %get-tuple-element.54), channel_id=1, source_target_pairs={{0,6},{1,7},{2,0},{3,1},{4,2},{5,3},{6,4},{7,5},{8,14},{9,15},{10,... | collective-permute-start | bytes 589832 | tf_op jit(solution)/shard_map/ppermute | solution.py:49
  208.3 5.3 %collective-permute-done.32.refs_0_ = bf16[128,768]{1,0:T(8,128)(2,1)S(1)} collective-permute-done((bf16[128,768]{1,0:T(8,128)(2,1)S(1)}, bf16[128,768]{1,0:T(8,128)(2,1)S(1)}, u32[]{:S(2)}, u32[]{:S(2)}) %collective-permute-start.32) | collective-permute-done | bytes 196640 | tf_op jit(solution)/shard_map/ppermute | solution.py:49
  214.1 1.6 collective-permute-done.34.refs_2_
  215.7 1.3 shard_map.74
  (111 shorter events, 19.9 us)
Async XLA Ops:
  0.0 12.8 %copy-start = (bf16[768,8]{0,1:T(8,128)(2,1)S(1)}, bf16[768,8]{0,1:T(8,128)(2,1)}, u32[]{:S(2)}) copy-start(bf16[768,8]{0,1:T(8,128)(2,1)} %param.7) | copy-start | bytes 36868
  0.8 11.9 %copy-start.9 = (bf16[128,768]{1,0:T(8,128)(2,1)S(1)}, bf16[128,768]{1,0:T(8,128)(2,1)}, u32[]{:S(2)}) copy-start(bf16[128,768]{1,0:T(8,128)(2,1)} %param.6) | copy-start | bytes 589828
  4.8 25.3 %all-to-all-start = ((bf16[16,56,768]{2,1,0:T(8,128)(2,1)}), bf16[16,56,768]{2,1,0:T(8,128)(2,1)S(1)}, u32[]{:S(2)}, u32[]{:S(2)}) async-start(bf16[16,56,768]{2,1,0:T(8,128)(2,1)} %bitcast.31), calls=%async_computation | async-start | bytes 2752512 | tf_op jit(solution)/shard_map/all_to_all | solution.py:341
  13.1 10.1 %collective-permute-start.2 = (bf16[128,896]{0,1:T(8,128)(2,1)S(1)}, bf16[128,896]{0,1:T(8,128)(2,1)S(1)}, u32[]{:S(2)}, u32[]{:S(2)}) collective-permute-start(bf16[128,896]{0,1:T(8,128)(2,1)S(1)} %broadcast_dynamic-update-slice_fusion), channel_id=1, source_target_pairs={{0,4},{1,5},{2,6},{3,7},{4,0},{5,1},{6,2},{7,3},{8,12},{9,13},{10,... | collective-permute-start | bytes 688136 | tf_op jit(solution)/shard_map/ppermute | solution.py:49
  16.3 10.4 %collective-permute-start.1 = (bf16[128,896]{0,1:T(8,128)(2,1)S(1)}, bf16[128,896]{0,1:T(8,128)(2,1)S(1)}, u32[]{:S(2)}, u32[]{:S(2)}) collective-permute-start(bf16[128,896]{0,1:T(8,128)(2,1)S(1)} %broadcast_dynamic-update-slice_fusion), channel_id=1, source_target_pairs={{0,6},{1,7},{2,0},{3,1},{4,2},{5,3},{6,4},{7,5},{8,14},{9,15},{10,... | collective-permute-start | bytes 688136 | tf_op jit(solution)/shard_map/ppermute | solution.py:49
  17.4 9.4 %collective-permute-start = (bf16[128,896]{0,1:T(8,128)(2,1)S(1)}, bf16[128,896]{0,1:T(8,128)(2,1)S(1)}, u32[]{:S(2)}, u32[]{:S(2)}) collective-permute-start(bf16[128,896]{0,1:T(8,128)(2,1)S(1)} %broadcast_dynamic-update-slice_fusion), channel_id=1, source_target_pairs={{0,2},{1,3},{2,4},{3,5},{4,6},{5,7},{6,0},{7,1},{8,10},{9,11},{10,... | collective-permute-start | bytes 688136 | tf_op jit(solution)/shard_map/ppermute | solution.py:49
  26.7 2.3 %copy-start.10 = (bf16[128,896]{0,1:T(8,128)(2,1)}, bf16[128,896]{0,1:T(8,128)(2,1)S(1)}, u32[]{:S(2)}) copy-start(bf16[128,896]{0,1:T(8,128)(2,1)S(1)} %collective-permute-done.1) | copy-start | bytes 688132
  26.8 2.3 %copy-start.11 = (bf16[128,896]{0,1:T(8,128)(2,1)}, bf16[128,896]{0,1:T(8,128)(2,1)S(1)}, u32[]{:S(2)}) copy-start(bf16[128,896]{0,1:T(8,128)(2,1)S(1)} %collective-permute-done) | copy-start | bytes 688132
  30.7 23.9 %collective-permute-start.18 = (bf16[504,768]{1,0:T(8,128)(2,1)S(1)}, bf16[504,768]{1,0:T(8,128)(2,1)}, u32[]{:S(2)}, u32[]{:S(2)}) collective-permute-start(bf16[504,768]{1,0:T(8,128)(2,1)S(1)} %bitcast.65), channel_id=1, source_target_pairs={{0,2},{1,3},{2,4},{3,5},{4,6},{5,7},{6,0},{7,1},{8,10},{9,11},{10,... | collective-permute-start | bytes 2322440 | tf_op jit(solution)/shard_map/ppermute | solution.py:49
  32.4 22.8 %collective-permute-start.20 = (bf16[504,768]{1,0:T(8,128)(2,1)S(1)}, bf16[504,768]{1,0:T(8,128)(2,1)}, u32[]{:S(2)}, u32[]{:S(2)}) collective-permute-start(bf16[504,768]{1,0:T(8,128)(2,1)S(1)} %bitcast.66), channel_id=1, source_target_pairs={{0,6},{1,7},{2,0},{3,1},{4,2},{5,3},{6,4},{7,5},{8,14},{9,15},{10,... | collective-permute-start | bytes 2322440 | tf_op jit(solution)/shard_map/ppermute | solution.py:49
  35.8 16.6 %collective-permute-start.4 = (bf16[56,3072]{1,0:T(8,128)(2,1)S(1)}, bf16[56,3072]{1,0:T(8,128)(2,1)S(1)}, u32[]{:S(2)}, u32[]{:S(2)}) collective-permute-start(bf16[56,3072]{1,0:T(8,128)(2,1)S(1)} %get-tuple-element.51), channel_id=1, source_target_pairs={{0,8},{8,16},{16,24},{24,0},{32,40},{40,48},{48,56},{56,32},{64,72... | collective-permute-start | bytes 1032200 | tf_op jit(solution)/shard_map/ppermute | solution.py:44
  38.0 16.7 %collective-permute-start.5 = (bf16[56,3072]{1,0:T(8,128)(2,1)S(1)}, bf16[56,3072]{1,0:T(8,128)(2,1)S(1)}, u32[]{:S(2)}, u32[]{:S(2)}) collective-permute-start(bf16[56,3072]{1,0:T(8,128)(2,1)S(1)} %get-tuple-element.50), channel_id=1, source_target_pairs={{0,24},{8,0},{16,8},{24,16},{32,56},{40,32},{48,40},{56,48},{64,88... | collective-permute-start | bytes 1032200 | tf_op jit(solution)/shard_map/ppermute | solution.py:44
  38.0 17.3 %collective-permute-start.6 = (bf16[56,3072]{1,0:T(8,128)(2,1)S(1)}, bf16[56,3072]{1,0:T(8,128)(2,1)S(1)}, u32[]{:S(2)}, u32[]{:S(2)}) collective-permute-start(bf16[56,3072]{1,0:T(8,128)(2,1)S(1)} %get-tuple-element.49), channel_id=1, source_target_pairs={{0,16},{8,24},{16,0},{24,8},{32,48},{40,56},{48,32},{56,40},{64,80... | collective-permute-start | bytes 1032200 | tf_op jit(solution)/shard_map/ppermute | solution.py:44
  52.4 8.7 %collective-permute-start.7 = (bf16[56,3072]{1,0:T(8,128)(2,1)S(1)}, bf16[56,3072]{1,0:T(8,128)(2,1)S(1)}, u32[]{:S(2)}, u32[]{:S(2)}) collective-permute-start(bf16[56,3072]{1,0:T(8,128)(2,1)S(1)} %get-tuple-element.48), channel_id=1, source_target_pairs={{0,32},{8,40},{16,48},{24,56},{32,64},{40,72},{48,80},{56,88},{64,... | collective-permute-start | bytes 1032200 | tf_op jit(solution)/shard_map/ppermute | solution.py:44
  54.6 27.2 %collective-permute-start.24 = (bf16[504,768]{1,0:T(8,128)(2,1)S(1)}, bf16[504,768]{1,0:T(8,128)(2,1)}, u32[]{:S(2)}, u32[]{:S(2)}) collective-permute-start(bf16[504,768]{1,0:T(8,128)(2,1)S(1)} %bitcast.67), channel_id=1, source_target_pairs={{0,1},{1,0},{2,3},{3,2},{4,5},{5,4},{6,7},{7,6},{8,9},{9,8},{10,11... | collective-permute-start | bytes 2322440 | tf_op jit(solution)/shard_map/ppermute | solution.py:53
  54.6 31.7 %collective-permute-start.25 = (bf16[504,768]{1,0:T(8,128)(2,1)}, bf16[504,768]{1,0:T(8,128)(2,1)}, u32[]{:S(2)}, u32[]{:S(2)}) collective-permute-start(bf16[504,768]{1,0:T(8,128)(2,1)} %collective-permute-done.18.refs_1_), channel_id=1, source_target_pairs={{0,1},{1,0},{2,3},{3,2},{4,5},{5,4},{6,7},{7,6},{8,9},{9,8},{10,11... | collective-permute-start | bytes 2322440 | tf_op jit(solution)/shard_map/ppermute | solution.py:53
  55.1 31.2 %collective-permute-start.26 = (bf16[504,768]{1,0:T(8,128)(2,1)}, bf16[504,768]{1,0:T(8,128)(2,1)}, u32[]{:S(2)}, u32[]{:S(2)}) collective-permute-start(bf16[504,768]{1,0:T(8,128)(2,1)} %collective-permute-done.20.refs_2_), channel_id=1, source_target_pairs={{0,1},{1,0},{2,3},{3,2},{4,5},{5,4},{6,7},{7,6},{8,9},{9,8},{10,11... | collective-permute-start | bytes 2322440 | tf_op jit(solution)/shard_map/ppermute | solution.py:53
  55.2 10.4 %collective-permute-start.8 = (bf16[56,3072]{1,0:T(8,128)(2,1)S(1)}, bf16[56,3072]{1,0:T(8,128)(2,1)S(1)}, u32[]{:S(2)}, u32[]{:S(2)}) collective-permute-start(bf16[56,3072]{1,0:T(8,128)(2,1)S(1)} %get-tuple-element.47), channel_id=1, source_target_pairs={{0,96},{8,104},{16,112},{24,120},{32,0},{40,8},{48,16},{56,24},{64... | collective-permute-start | bytes 1032200 | tf_op jit(solution)/shard_map/ppermute | solution.py:44
  61.2 12.4 %collective-permute-start.9 = (bf16[56,3072]{1,0:T(8,128)(2,1)S(1)}, bf16[56,3072]{1,0:T(8,128)(2,1)S(1)}, u32[]{:S(2)}, u32[]{:S(2)}) collective-permute-start(bf16[56,3072]{1,0:T(8,128)(2,1)S(1)} %get-tuple-element.46), channel_id=1, source_target_pairs={{0,64},{8,72},{16,80},{24,88},{32,96},{40,104},{48,112},{56,120},{... | collective-permute-start | bytes 1032200 | tf_op jit(solution)/shard_map/ppermute | solution.py:44
  66.4 19.4 %collective-permute-start.21 = (bf16[264,768]{1,0:T(8,128)(2,1)}, bf16[264,768]{1,0:T(8,128)(2,1)S(1)}, u32[]{:S(2)}, u32[]{:S(2)}) collective-permute-start(bf16[264,768]{1,0:T(8,128)(2,1)} %slice.199), channel_id=1, source_target_pairs={{0,6},{1,7},{2,0},{3,1},{4,2},{5,3},{6,4},{7,5},{8,14},{9,15},{10,... | collective-permute-start | bytes 1216520 | tf_op jit(solution)/shard_map/ppermute | solution.py:49
  74.3 11.5 %collective-permute-start.19 = (bf16[240,768]{1,0:T(8,128)(2,1)}, bf16[240,768]{1,0:T(8,128)(2,1)S(1)}, u32[]{:S(2)}, u32[]{:S(2)}) collective-permute-start(bf16[240,768]{1,0:T(8,128)(2,1)} %slice.198), channel_id=1, source_target_pairs={{0,2},{1,3},{2,4},{3,5},{4,6},{5,7},{6,0},{7,1},{8,10},{9,11},{10,... | collective-permute-start | bytes 1105928 | tf_op jit(solution)/shard_map/ppermute | solution.py:49
  74.5 6.6 %copy-start.6 = (bf16[56,3072]{1,0:T(8,128)(2,1)S(1)}, bf16[56,3072]{1,0:T(8,128)(2,1)}, u32[]{:S(2)}) copy-start(bf16[56,3072]{1,0:T(8,128)(2,1)} %copy-done.5) | copy-start | bytes 1032196
  74.5 6.6 %copy-start.8 = (bf16[56,3072]{1,0:T(8,128)(2,1)S(1)}, bf16[56,3072]{1,0:T(8,128)(2,1)}, u32[]{:S(2)}) copy-start(bf16[56,3072]{1,0:T(8,128)(2,1)} %copy-done.7) | copy-start | bytes 1032196
  81.8 21.6 %collective-permute-start.10 = (bf16[392,3072]{1,0:T(8,128)(2,1)S(1)}, bf16[392,3072]{1,0:T(8,128)(2,1)S(1)}, u32[]{:S(2)}, u32[]{:S(2)}) collective-permute-start(bf16[392,3072]{1,0:T(8,128)(2,1)S(1)} %bitcast.60), channel_id=1, source_target_pairs={{0,1},{1,0},{2,3},{3,2},{4,5},{5,4},{6,7},{7,6},{8,9},{9,8},{10,11... | collective-permute-start | bytes 7225352 | tf_op jit(solution)/shard_map/ppermute | solution.py:53
  85.8 7.6 %collective-permute-start.22 = (bf16[240,768]{1,0:T(8,128)(2,1)S(1)}, bf16[240,768]{1,0:T(8,128)(2,1)S(1)}, u32[]{:S(2)}, u32[]{:S(2)}) collective-permute-start(bf16[240,768]{1,0:T(8,128)(2,1)S(1)} %collective-permute-done.19.refs_0_), channel_id=1, source_target_pairs={{0,1},{1,0},{2,3},{3,2},{4,5},{5,4},{6,7},{7,6},{8,9},{9,8},{10,11... | collective-permute-start | bytes 1105928 | tf_op jit(solution)/shard_map/ppermute | solution.py:53
  85.8 7.6 %collective-permute-start.23 = (bf16[264,768]{1,0:T(8,128)(2,1)S(1)}, bf16[264,768]{1,0:T(8,128)(2,1)S(1)}, u32[]{:S(2)}, u32[]{:S(2)}) collective-permute-start(bf16[264,768]{1,0:T(8,128)(2,1)S(1)} %collective-permute-done.21.refs_1_), channel_id=1, source_target_pairs={{0,1},{1,0},{2,3},{3,2},{4,5},{5,4},{6,7},{7,6},{8,9},{9,8},{10,11... | collective-permute-start | bytes 1216520 | tf_op jit(solution)/shard_map/ppermute | solution.py:53
  100.1 16.6 %collective-permute-start.27 = (bf16[4,504,768]{2,1,0:T(8,128)(2,1)S(1)}, bf16[4,504,768]{2,1,0:T(8,128)(2,1)S(1)}, u32[]{:S(2)}, u32[]{:S(2)}) collective-permute-start(bf16[4,504,768]{2,1,0:T(8,128)(2,1)S(1)} %get-tuple-element.29), channel_id=1, source_target_pairs={{0,1},{1,0},{2,3},{3,2},{4,5},{5,4},{6,7},{7,6},{8,9},{9,8},{10,11... | collective-permute-start | bytes 9289736 | tf_op jit(solution)/shard_map/ppermute | solution.py:53
  111.0 5.7 %copy-start.2 = (bf16[4,392,768]{2,1,0:T(8,128)(2,1)}, bf16[4,392,768]{2,1,0:T(8,128)(2,1)S(1)}, u32[]{:S(2)}) copy-start(bf16[4,392,768]{2,1,0:T(8,128)(2,1)S(1)} %get-tuple-element.23) | copy-start | bytes 7225348
  111.0 25.1 %collective-permute-start.11 = (bf16[4,392,768]{2,1,0:T(8,128)(2,1)}, bf16[4,392,768]{2,1,0:T(8,128)(2,1)}, u32[]{:S(2)}, u32[]{:S(2)}) collective-permute-start(bf16[4,392,768]{2,1,0:T(8,128)(2,1)} %get-tuple-element.24), channel_id=1, source_target_pairs={{0,1},{1,0},{2,3},{3,2},{4,5},{5,4},{6,7},{7,6},{8,9},{9,8},{10,11... | collective-permute-start | bytes 7225352 | tf_op jit(solution)/shard_map/ppermute | solution.py:53
  117.1 12.1 %collective-permute-start.30 = (bf16[264,768]{1,0:T(8,128)(2,1)S(1)}, bf16[264,768]{1,0:T(8,128)(2,1)S(1)}, u32[]{:S(2)}, u32[]{:S(2)}) collective-permute-start(bf16[264,768]{1,0:T(8,128)(2,1)S(1)} %slice_bitcast_fusion), channel_id=1, source_target_pairs={{0,6},{1,7},{2,0},{3,1},{4,2},{5,3},{6,4},{7,5},{8,14},{9,15},{10,... | collective-permute-start | bytes 1216520 | tf_op jit(solution)/shard_map/ppermute | solution.py:49
  117.6 18.4 %copy-start.12 = (s32[128,2]{0,1:T(2,128)S(1)}, s32[128,2]{0,1:T(2,128)}, u32[]{:S(2)}) copy-start(s32[128,2]{0,1:T(2,128)} %param.8) | copy-start | bytes 3076
  117.6 11.5 %collective-permute-start.28 = (bf16[240,768]{1,0:T(8,128)(2,1)S(1)}, bf16[240,768]{1,0:T(8,128)(2,1)S(1)}, u32[]{:S(2)}, u32[]{:S(2)}) collective-permute-start(bf16[240,768]{1,0:T(8,128)(2,1)S(1)} %slice_bitcast_fusion.1), channel_id=1, source_target_pairs={{0,2},{1,3},{2,4},{3,5},{4,6},{5,7},{6,0},{7,1},{8,10},{9,11},{10,... | collective-permute-start | bytes 1105928 | tf_op jit(solution)/shard_map/ppermute | solution.py:49
  130.9 19.5 %collective-permute-start.29 = (bf16[504,768]{1,0:T(8,128)(2,1)}, bf16[504,768]{1,0:T(8,128)(2,1)S(1)}, u32[]{:S(2)}, u32[]{:S(2)}) collective-permute-start(bf16[504,768]{1,0:T(8,128)(2,1)} %get-tuple-element.36), channel_id=1, source_target_pairs={{0,2},{1,3},{2,4},{3,5},{4,6},{5,7},{6,0},{7,1},{8,10},{9,11},{10,... | collective-permute-start | bytes 2322440 | tf_op jit(solution)/shard_map/ppermute | solution.py:49
  131.2 20.0 %collective-permute-start.31 = (bf16[504,768]{1,0:T(8,128)(2,1)}, bf16[504,768]{1,0:T(8,128)(2,1)}, u32[]{:S(2)}, u32[]{:S(2)}) collective-permute-start(bf16[504,768]{1,0:T(8,128)(2,1)} %get-tuple-element.35), channel_id=1, source_target_pairs={{0,6},{1,7},{2,0},{3,1},{4,2},{5,3},{6,4},{7,5},{8,14},{9,15},{10,... | collective-permute-start | bytes 2322440 | tf_op jit(solution)/shard_map/ppermute | solution.py:49
  134.8 1.2 collective-permute-start.3
  150.3 0.9 copy-start.3
  151.2 1.1 copy-start.4
  154.9 60.8 %all-to-all-start.1 = ((bf16[16,56,768]{2,1,0:T(8,128)(2,1)}), bf16[16,56,768]{2,1,0:T(8,128)(2,1)S(1)}, u32[]{:S(2)}, u32[]{:S(2)}) async-start(bf16[16,56,768]{2,1,0:T(8,128)(2,1)} %shard_map.73), calls=%async_computation.1 | async-start | bytes 2752512 | tf_op jit(solution)/shard_map/all_to_all | solution.py:422
  167.6 23.8 %collective-permute-start.12 = (bf16[4,56,768]{2,1,0:T(8,128)(2,1)S(1)}, bf16[4,56,768]{2,1,0:T(8,128)(2,1)S(1)}, u32[]{:S(2)}, u32[]{:S(2)}) collective-permute-start(bf16[4,56,768]{2,1,0:T(8,128)(2,1)S(1)} %get-tuple-element.44), channel_id=1, source_target_pairs={{0,24},{8,0},{16,8},{24,16},{32,56},{40,32},{48,40},{56,48},{64,88... | collective-permute-start | bytes 1032200 | tf_op jit(solution)/shard_map/ppermute | solution.py:44
  168.4 25.6 %collective-permute-start.13 = (bf16[4,56,768]{2,1,0:T(8,128)(2,1)S(1)}, bf16[4,56,768]{2,1,0:T(8,128)(2,1)S(1)}, u32[]{:S(2)}, u32[]{:S(2)}) collective-permute-start(bf16[4,56,768]{2,1,0:T(8,128)(2,1)S(1)} %get-tuple-element.43), channel_id=1, source_target_pairs={{0,8},{8,16},{16,24},{24,0},{32,40},{40,48},{48,56},{56,32},{64,72... | collective-permute-start | bytes 1032200 | tf_op jit(solution)/shard_map/ppermute | solution.py:44
  170.0 26.3 %collective-permute-start.14 = (bf16[4,56,768]{2,1,0:T(8,128)(2,1)S(1)}, bf16[4,56,768]{2,1,0:T(8,128)(2,1)S(1)}, u32[]{:S(2)}, u32[]{:S(2)}) collective-permute-start(bf16[4,56,768]{2,1,0:T(8,128)(2,1)S(1)} %get-tuple-element.42), channel_id=1, source_target_pairs={{0,16},{8,24},{16,0},{24,8},{32,48},{40,56},{48,32},{56,40},{64,80... | collective-permute-start | bytes 1032200 | tf_op jit(solution)/shard_map/ppermute | solution.py:44
  173.2 23.0 %collective-permute-start.15 = (bf16[4,56,768]{2,1,0:T(8,128)(2,1)S(1)}, bf16[4,56,768]{2,1,0:T(8,128)(2,1)S(1)}, u32[]{:S(2)}, u32[]{:S(2)}) collective-permute-start(bf16[4,56,768]{2,1,0:T(8,128)(2,1)S(1)} %get-tuple-element.41), channel_id=1, source_target_pairs={{0,96},{8,104},{16,112},{24,120},{32,0},{40,8},{48,16},{56,24},{64... | collective-permute-start | bytes 1032200 | tf_op jit(solution)/shard_map/ppermute | solution.py:44
  173.8 22.5 %collective-permute-start.16 = (bf16[4,56,768]{2,1,0:T(8,128)(2,1)S(1)}, bf16[4,56,768]{2,1,0:T(8,128)(2,1)S(1)}, u32[]{:S(2)}, u32[]{:S(2)}) collective-permute-start(bf16[4,56,768]{2,1,0:T(8,128)(2,1)S(1)} %get-tuple-element.40), channel_id=1, source_target_pairs={{0,32},{8,40},{16,48},{24,56},{32,64},{40,72},{48,80},{56,88},{64,... | collective-permute-start | bytes 1032200 | tf_op jit(solution)/shard_map/ppermute | solution.py:44
  191.4 10.2 %collective-permute-start.17 = (bf16[4,56,768]{2,1,0:T(8,128)(2,1)S(1)}, bf16[4,56,768]{2,1,0:T(8,128)(2,1)S(1)}, u32[]{:S(2)}, u32[]{:S(2)}) collective-permute-start(bf16[4,56,768]{2,1,0:T(8,128)(2,1)S(1)} %get-tuple-element.39), channel_id=1, source_target_pairs={{0,64},{8,72},{16,80},{24,88},{32,96},{40,104},{48,112},{56,120},{... | collective-permute-start | bytes 1032200 | tf_op jit(solution)/shard_map/ppermute | solution.py:44
  204.6 12.4 %copy-start.1 = (bf16[768,8]{0,1:T(8,128)(2,1)S(1)}, bf16[768,8]{0,1:T(8,128)(2,1)}, u32[]{:S(2)}) copy-start(bf16[768,8]{0,1:T(8,128)(2,1)} %param.7) | copy-start | bytes 36868
  204.7 8.9 %collective-permute-start.32 = (bf16[128,768]{1,0:T(8,128)(2,1)S(1)}, bf16[128,768]{1,0:T(8,128)(2,1)S(1)}, u32[]{:S(2)}, u32[]{:S(2)}) collective-permute-start(bf16[128,768]{1,0:T(8,128)(2,1)S(1)} %get-tuple-element.55), channel_id=1, source_target_pairs={{0,2},{1,3},{2,4},{3,5},{4,6},{5,7},{6,0},{7,1},{8,10},{9,11},{10,... | collective-permute-start | bytes 589832 | tf_op jit(solution)/shard_map/ppermute | solution.py:49
  204.7 9.3 %collective-permute-start.33 = (bf16[128,768]{1,0:T(8,128)(2,1)S(1)}, bf16[128,768]{1,0:T(8,128)(2,1)S(1)}, u32[]{:S(2)}, u32[]{:S(2)}) collective-permute-start(bf16[128,768]{1,0:T(8,128)(2,1)S(1)} %get-tuple-element.54), channel_id=1, source_target_pairs={{0,6},{1,7},{2,0},{3,1},{4,2},{5,3},{6,4},{7,5},{8,14},{9,15},{10,... | collective-permute-start | bytes 589832 | tf_op jit(solution)/shard_map/ppermute | solution.py:49
  208.0 7.7 %collective-permute-start.34 = (bf16[128,768]{1,0:T(8,128)(2,1)S(1)}, bf16[128,768]{1,0:T(8,128)(2,1)S(1)}, u32[]{:S(2)}, u32[]{:S(2)}) collective-permute-start(bf16[128,768]{1,0:T(8,128)(2,1)S(1)} %get-tuple-element.53), channel_id=1, source_target_pairs={{0,4},{1,5},{2,6},{3,7},{4,0},{5,1},{6,2},{7,3},{8,12},{9,13},{10,... | collective-permute-start | bytes 589832 | tf_op jit(solution)/shard_map/ppermute | solution.py:49
  (2 other events, 1.5 us)

commit v2 on v1

--- a/solution.py
+++ b/solution.py
@@ -106,19 +106,21 @@
     )(where, *[in_vmem(x) for x in xs], gate_slab, up_slab)
 
 
-def down_blocks(where, hid, down_w, target, first, obuf, sem):
+def down_blocks(where, hid, down_w, target, other, rels, obuf, sem, first=0):
     stores = []
-    for rel in range(4):
-        obuf[first + rel] = bf16(dot(hid, down_w[:, pl.ds(block_start(where, first + rel), BLK)]))
-        copy = pltpu.make_async_copy(obuf.at[first + rel], target.at[rel], sem.at[first + rel])
+    for i, rel in enumerate(rels):
+        cut = pl.ds(block_start(where, 4 * other + rel), BLK)
+        obuf[first + i] = bf16(dot(hid, down_w[:, cut]))
+        copy = pltpu.make_async_copy(obuf.at[first + i], target.at[i], sem.at[first + i])
         copy.start()
         stores.append(copy)
     return stores
 
 
-def expert(where, xs, pieces, rows, gate_slab, up_slab, down_slab, sums, whole):
+def expert(where, xs, pieces, rows, gate_slab, up_slab, down_slab, sums, rels, whole):
     ffn = gate_slab.shape[1]
     count = len(xs)
+    width = len(rels)
 
     def body(where, *refs):
         xs_w, refs = refs[: count + 2], refs[count + 2 :]
@@ -130,13 +132,13 @@
         gate_body(pieces, count, True, where, (*xs_w, *given, gacc, uacc))
         gate = gacc[...]
         hid[...] = bf16(gate / (1.0 + jnp.exp(-gate)) * uacc[...])
-        stores = down_blocks(where, hid[...], down_w, send, 4, obuf, sem)
+        stores = down_blocks(where, hid[...], down_w, send, 1, rels, obuf, sem)
         if whole:
-            stores = stores + down_blocks(where, hid[...], down_w, keep, 0, obuf, sem)
+            stores = stores + down_blocks(where, hid[...], down_w, keep, 0, rels, obuf, sem, width)
         for copy in stores:
             copy.wait()
 
-    out = jax.ShapeDtypeStruct((4, rows, BLK), jnp.bfloat16)
+    out = jax.ShapeDtypeStruct((width, rows, BLK), jnp.bfloat16)
     hidden = jax.ShapeDtypeStruct((rows, ffn), jnp.bfloat16)
     scratch = [pltpu.VMEM((rows, ffn), jnp.float32), pltpu.VMEM((rows, ffn), jnp.float32)]
     if whole:
@@ -148,8 +150,8 @@
         out_specs=(ANY_SPEC, ANY_SPEC if whole else VMEM_SPEC),
         scratch_shapes=[
             *scratch,
-            pltpu.VMEM((8, rows, BLK), jnp.bfloat16),
-            pltpu.SemaphoreType.DMA((8,)),
+            pltpu.VMEM((2 * width, rows, BLK), jnp.bfloat16),
+            pltpu.SemaphoreType.DMA((2 * width,)),
         ],
         compiler_params=pltpu.CompilerParams(vmem_limit_bytes=20 * 1024 * 1024),
         cost_estimate=cost(rows, ffn, 0.5),
@@ -163,24 +165,25 @@
     )
 
 
-def down_part(where, hid, down_slab):
+def down_part(where, hid, down_slab, other, rels):
     rows, ffn = hid.shape
-
-    def body(where, hid, down_w, keep, obuf, sem):
-        for copy in down_blocks(where, hid[...], down_w, keep, 0, obuf, sem):
+    width = len(rels)
+
+    def body(where, hid, down_w, out, obuf, sem):
+        for copy in down_blocks(where, hid[...], down_w, out, other, rels, obuf, sem):
             copy.wait()
 
     return pl.pallas_call(
         body,
-        out_shape=jax.ShapeDtypeStruct((4, rows, BLK), jnp.bfloat16),
+        out_shape=jax.ShapeDtypeStruct((width, rows, BLK), jnp.bfloat16),
         in_specs=[SMEM_SPEC, VMEM_SPEC, VMEM_SPEC],
         out_specs=ANY_SPEC,
         scratch_shapes=[
-            pltpu.VMEM((4, rows, BLK), jnp.bfloat16),
-            pltpu.SemaphoreType.DMA((4,)),
+            pltpu.VMEM((width, rows, BLK), jnp.bfloat16),
+            pltpu.SemaphoreType.DMA((width,)),
         ],
         compiler_params=pltpu.CompilerParams(vmem_limit_bytes=10 * 1024 * 1024),
-        cost_estimate=cost(rows, ffn, 0.2),
+        cost_estimate=cost(rows, ffn, 0.05 * width),
     )(where, in_vmem(hid), down_slab)
 
 
@@ -313,16 +316,11 @@
     def place(shift, sign=1):
         return (z_here + sign * shift[0]) % 4 * 4 + (x_here + sign * shift[1]) % 4
 
-    logits = dot(tokens, router_weight)
-    terms = []
-    rest = logits
-    for _ in range(3):
-        term = lax.reduce_precision(rest, 8, 7)
-        terms.append(bf16(term))
-        rest = rest - term
-    pad = jnp.zeros((tok_rows, 128 - 3 * experts), jnp.bfloat16)
-    packed = jnp.concatenate([tokens, jnp.concatenate(terms + [pad], axis=1)], axis=1)
-    gathered = [packed] + [y_shift(packed, step) for step in (1, 3, 2)]
+    gathered = [tokens] + [y_shift(tokens, step) for step in (1, 3, 2)]
+    partial = dot(tokens, router_weight)
+    logits = partial
+    for step in (1, 3, 2):
+        logits = logits + y_shift(partial, step)
 
     flat_ids = expert_ids.reshape(-1)
     total = tok_rows * top_count
@@ -345,7 +343,7 @@
     own = placed(sources, [received], [(0, -1 - i, i) for i in range(count)], count)
     own = own.reshape(far_rows, BLK)
 
-    full = jnp.concatenate([a[:, :BLK] for a in gathered], axis=1)
+    full = jnp.concatenate(gathered, axis=1)
     slot_index = jnp.arange(CAP, dtype=jnp.int32)
     near_keys = jnp.stack([place(k) // 2 for k in NEAR])[:, None] * CAP + slot_index[None, :]
     matches = jnp.any(near_keys.reshape(-1)[:, None, None] == token_keys[None], axis=2)
@@ -356,11 +354,7 @@
     near_in = near_in.reshape(near_rows, 4 * BLK)
     near_other = core_swap(near_in)
 
-    half_sum = jnp.zeros((tok_rows, experts), jnp.float32)
-    for a in gathered:
-        for i in range(3):
-            half_sum = half_sum + f32(a[:, BLK + i * experts : BLK + (i + 1) * experts])
-    logits = half_sum + core_swap(half_sum)
+    logits = logits + core_swap(logits)
     chosen = expert_ids[:, :, None] == jnp.arange(experts, dtype=jnp.int32)[None, None, :]
     picked = jnp.sum(jnp.where(chosen, logits[:, None, :], 0.0), axis=2)
     gates = jax.nn.sigmoid(picked - picked[:, ::-1])
@@ -374,7 +368,7 @@
     pieces = [(rel, 0, lane * BLK, 0, near_rows) for lane, rel in enumerate(RELS)]
     sums = gate_part(where, [near_in], pieces, near_rows, *slabs[:2])
     pieces = [(4 + rel, 0, lane * BLK, 0, near_rows) for lane, rel in enumerate(RELS)]
-    send, keep = expert(where, [near_other], pieces, near_rows, *slabs, sums, True)
+    send, keep = expert(where, [near_other], pieces, near_rows, *slabs, sums, (0, 1, 2, 3), True)
     got = core_swap(send)
     summed = bf16(f32(keep) + f32(got))
     returned = []
@@ -403,16 +397,19 @@
     for other in range(2):
         pieces.append((4 * other + 2, 2 * other, 0, 0, cut))
         pieces.append((4 * other + 2, 2 * other + 1, 0, cut, far_rows - cut))
-    send, hid = expert(where, last, pieces, far_rows, *slabs, sums, False)
+    send, hid = expert(where, last, pieces, far_rows, *slabs, sums, (2,), False)
     got = core_swap(send)
-    keep = down_part(where, hid, slabs[2])
-    across_sum = bf16(f32(keep[2]) + f32(got[2]))
+    keep = down_part(where, hid, slabs[2], 0, (2,))
+    across_sum = bf16(f32(keep[0]) + f32(got[0]))
+    send = down_part(where, hid, slabs[2], 1, (0, 1, 3))
+    got = core_swap(send)
+    keep = down_part(where, hid, slabs[2], 0, (0, 1, 3))
     from_below = y_shift(across_sum[:cut], 1)
     from_above = y_shift(across_sum[cut:], 3)
     zero_low = jnp.zeros((far_rows - cut, BLK), jnp.float32)
     zero_high = jnp.zeros((cut, BLK), jnp.float32)
     to_above = f32(keep[1]) + f32(got[1]) + jnp.concatenate([f32(from_below), zero_low], axis=0)
-    to_below = f32(keep[3]) + f32(got[3]) + jnp.concatenate([zero_high, f32(from_above)], axis=0)
+    to_below = f32(keep[2]) + f32(got[2]) + jnp.concatenate([zero_high, f32(from_above)], axis=0)
     shape = (count, CAP, BLK)
     homes = jnp.stack([place(k, -1) for k in FAR + NEAR]).astype(jnp.int32)
     base = (f32(keep[0]) + f32(got[0])).reshape(shape)

time: 218 us -> 215 us (0.986)
  the two profiles are of different devices: /device:TPU:34 before, /device:TPU:2 now
where the time goes in v2:
time: 215 us; the launch traced here: 214 us
  waiting for transfers between devices  81.3 us (38%)
  starting transfers between devices  61.8 us (29%)
  Pallas kernels  43 us (20%)
  local copies, waits for them, and re-layouts  13.9 us (6%)
  other arithmetic  10.3 us (5%)
  matrix products  3.71 us (2%)
    ppermute x12, waiting for transfers between devices, seq_shift(): return lax.ppermute(array, 'seq', pairs)  40.2 us
    ppermute x17, waiting for transfers between devices, y_shift(): return lax.ppermute(array, 'tp', pairs)  26.2 us
    ppermute x17, starting transfers between devices, y_shift(): return lax.ppermute(array, 'tp', pairs)  23.1 us
    ppermute x12, starting transfers between devices, seq_shift(): return lax.ppermute(array, 'seq', pairs)  20.2 us
    all_to_all x1, waiting for transfers between devices, layer(): received = lax.all_to_all(out, 'seq', 0, 0, tiled=True)  13.9 us
    pallas_call x2, Pallas kernels, expert(): pl.pallas_call(body, out_shape=(out, out if whole else hidden), in_specs=...  10.8 us
    pallas_call x2, Pallas kernels, gate_part(): pl.pallas_call(body, out_shape=(out, out), in_specs=[SMEM_SPEC] + [VMEM_S...  9.65 us
    all_to_all x1, starting transfers between devices, layer(): received = lax.all_to_all(out, 'seq', 0, 0, tiled=True)  8.32 us
  transfers between devices with their start and end apart: 41, of which 17 were waited for; matrix products, arithmetic and copies ran while one was open for 10% of the time, Pallas kernels for 18%

profile of v2, /device:TPU:2, one launch (start us, length us, event | category | flops | bytes accessed | tf_op | source)
XLA Modules:
  0.0 214.5 jit_solution(17355217600567069826)
XLA Ops:
  0.0 3.2 %collective-permute-start.6 = (bf16[128,768]{1,0:T(8,128)(2,1)}, bf16[128,768]{1,0:T(8,128)(2,1)S(1)}, u32[]{:S(2)}, u32[]{:S(2)}) collective-permute-start(bf16[128,768]{1,0:T(8,128)(2,1)} %param.6), channel_id=1, source_target_pairs={{0,4},{1,5},{2,6},{3,7},{4,0},{5,1},{6,2},{7,3},{8,12},{9,13},{10,... | collective-permute-start | bytes 589832 | tf_op jit(solution)/shard_map/ppermute | solution.py:49
  7.5 2.6 %convolution_convert_fusion.1 = bf16[896,768]{1,0:T(8,128)(2,1)} fusion(pred[896,128]{1,0:T(8,128)(4,1)S(1)} %compare_reduce_fusion, bf16[128,768]{1,0:T(8,128)(2,1)} %param.6), kind=kOutput, calls=%fused_computation.2 | convolution fusion | flops 176848896 | bytes 1687552 | tf_op jit(solution)/shard_map/dot_general | solution.py:29
  10.1 8.3 %all-to-all-start = ((bf16[16,56,768]{2,1,0:T(8,128)(2,1)}), bf16[16,56,768]{2,1,0:T(8,128)(2,1)S(1)}, u32[]{:S(2)}, u32[]{:S(2)}) async-start(bf16[16,56,768]{2,1,0:T(8,128)(2,1)} %bitcast.31), calls=%async_computation | async-start | bytes 2752512 | tf_op jit(solution)/shard_map/all_to_all | solution.py:339
  19.6 1.3 fusion.29
  21.0 1.5 collective-permute-start.7
  23.0 2.1 collective-permute-start.9
  25.2 13.9 %all-to-all-done.refs_0_ = bf16[16,56,768]{2,1,0:T(8,128)(2,1)S(1)} async-done(((bf16[16,56,768]{2,1,0:T(8,128)(2,1)}), bf16[16,56,768]{2,1,0:T(8,128)(2,1)S(1)}, u32[]{:S(2)}, u32[]{:S(2)}) %all-to-all-start) | async-done | bytes 1376288 | tf_op jit(solution)/shard_map/all_to_all | solution.py:339
  40.5 2.6 %collective-permute-start.23 = (bf16[504,768]{1,0:T(8,128)(2,1)S(1)}, bf16[504,768]{1,0:T(8,128)(2,1)}, u32[]{:S(2)}, u32[]{:S(2)}) collective-permute-start(bf16[504,768]{1,0:T(8,128)(2,1)S(1)} %bitcast.66), channel_id=1, source_target_pairs={{0,6},{1,7},{2,0},{3,1},{4,2},{5,3},{6,4},{7,5},{8,14},{9,15},{10,... | collective-permute-start | bytes 2322440 | tf_op jit(solution)/shard_map/ppermute | solution.py:49
  43.0 5.2 %collective-permute-done.7.refs_1_ = bf16[56,3072]{1,0:T(8,128)(2,1)S(1)} collective-permute-done((bf16[56,3072]{1,0:T(8,128)(2,1)}, bf16[56,3072]{1,0:T(8,128)(2,1)S(1)}, u32[]{:S(2)}, u32[]{:S(2)}) %collective-permute-start.7) | collective-permute-done | bytes 344096 | tf_op jit(solution)/shard_map/ppermute | solution.py:44
  48.2 3.2 %collective-permute-start.11 = (bf16[56,3072]{1,0:T(8,128)(2,1)}, bf16[56,3072]{1,0:T(8,128)(2,1)S(1)}, u32[]{:S(2)}, u32[]{:S(2)}) collective-permute-start(bf16[56,3072]{1,0:T(8,128)(2,1)} %get-tuple-element.45), channel_id=1, source_target_pairs={{0,96},{8,104},{16,112},{24,120},{32,0},{40,8},{48,16},{56,24},{64... | collective-permute-start | bytes 1032200 | tf_op jit(solution)/shard_map/ppermute | solution.py:44
  51.5 1.8 collective-permute-start.12
  53.3 7.3 %collective-permute-done.10.refs_4_ = bf16[56,3072]{1,0:T(8,128)(2,1)S(1)} collective-permute-done((bf16[56,3072]{1,0:T(8,128)(2,1)}, bf16[56,3072]{1,0:T(8,128)(2,1)S(1)}, u32[]{:S(2)}, u32[]{:S(2)}) %collective-permute-start.10) | collective-permute-done | bytes 344096 | tf_op jit(solution)/shard_map/ppermute | solution.py:44
  60.7 5.7 %collective-permute-done.11.refs_5_ = bf16[56,3072]{1,0:T(8,128)(2,1)S(1)} collective-permute-done((bf16[56,3072]{1,0:T(8,128)(2,1)}, bf16[56,3072]{1,0:T(8,128)(2,1)S(1)}, u32[]{:S(2)}, u32[]{:S(2)}) %collective-permute-start.11) | collective-permute-done | bytes 344096 | tf_op jit(solution)/shard_map/ppermute | solution.py:44
  69.5 2.3 %collective-permute-start.24 = (bf16[264,768]{1,0:T(8,128)(2,1)S(1)}, bf16[264,768]{1,0:T(8,128)(2,1)S(1)}, u32[]{:S(2)}, u32[]{:S(2)}) collective-permute-start(bf16[264,768]{1,0:T(8,128)(2,1)S(1)} %slice.131), channel_id=1, source_target_pairs={{0,6},{1,7},{2,0},{3,1},{4,2},{5,3},{6,4},{7,5},{8,14},{9,15},{10,... | collective-permute-start | bytes 1216520 | tf_op jit(solution)/shard_map/ppermute | solution.py:49
  73.0 6.4 %shard_map.65 = (bf16[6144,512]{1,0:T(8,128)(2,1)S(1)}, bf16[6144,512]{1,0:T(8,128)(2,1)S(1)}, bf16[512,6144]{1,0:T(8,128)(2,1)S(1)}) custom-call(bf16[6144,512]{1,0:T(8,128)(2,1)} %bitcast.69, bf16[6144,512]{1,0:T(8,128)(2,1)} %bitcast.70, bf16[512,6144]{1,0:T(8,128)(2,1)} %bitcast.71), custom_call_target="tpu_custom_call" | custom-call | tf_op jit(solution)/shard_map/pallas_call | solution.py:224
  79.4 5.4 %collective-permute-done.22.refs_0_ = bf16[240,768]{1,0:T(8,128)(2,1)S(1)} collective-permute-done((bf16[240,768]{1,0:T(8,128)(2,1)S(1)}, bf16[240,768]{1,0:T(8,128)(2,1)S(1)}, u32[]{:S(2)}, u32[]{:S(2)}) %collective-permute-start.22) | collective-permute-done | bytes 368672 | tf_op jit(solution)/shard_map/ppermute | solution.py:49
  85.3 6.4 %shard_map.70 = (f32[504,512]{1,0:T(8,128)S(1)}, f32[504,512]{1,0:T(8,128)S(1)}) custom-call(s32[2]{0:T(128)S(1)} %pad_add_fusion.places.where, bf16[504,768]{1,0:T(8,128)(2,1)S(1)} %bitcast.68, bf16[504,768]{1,0:T(8,128)(2,1)} %collective-permute-done.21.refs_1_, bf16[504,768]{1,0:T(8,128)(2,1)} %collective-permute-done.23.refs_2_, ...), custom_call_target="tpu_custom_call" | custom-call | flops 4756340736 | bytes 18874368 | tf_op jit(solution)/shard_map/pallas_call | solution.py:99
  91.7 3.3 %shard_map.71 = (bf16[1,504,768]{2,1,0:T(8,128)(2,1)S(1)}, bf16[504,512]{1,0:T(8,128)(2,1)S(1)}) custom-call(s32[2]{0:T(128)S(1)} %pad_add_fusion.places.where, bf16[240,768]{1,0:T(8,128)(2,1)S(1)} %collective-permute-done.22.refs_0_, bf16[264,768]{1,0:T(8,128)(2,1)S(1)} %collective-permute-done.24.refs_1_, ...), custom_call_target="tpu_custom_call" | custom-call | flops 4756340736 | bytes 18874368 | tf_op jit(solution)/shard_map/pallas_call | solution.py:146
  95.0 2.9 %shard_map.73 = bf16[3,504,768]{2,1,0:T(8,128)(2,1)} custom-call(s32[2]{0:T(128)S(1)} %pad_add_fusion.places.where, bf16[504,512]{1,0:T(8,128)(2,1)S(1)} %get-tuple-element.28.hid, bf16[512,6144]{1,0:T(8,128)(2,1)S(1)} %get-tuple-element.20.refs_3_.refs_6_.down_w), custom_call_target="tpu_custom_call" | custom-call | flops 1426902272 | bytes 18874368 | tf_op jit(solution)/shard_map/pallas_call | solution.py:176
  98.0 3.2 %shard_map.66 = (f32[392,512]{1,0:T(8,128)S(1)}, f32[392,512]{1,0:T(8,128)S(1)}) custom-call(s32[2]{0:T(128)S(1)} %pad_add_fusion.places.where, bf16[392,3072]{1,0:T(8,128)(2,1)S(1)} %bitcast.61, bf16[6144,512]{1,0:T(8,128)(2,1)S(1)} %get-tuple-element.18.refs_1_.refs_6_.refs_4_, bf16[6144,512]{1,0:T(8,128)(2,1)S(1)} %get-tuple-element.19.refs_2_.refs_7_.refs_5_), custom_call_target="tpu_custom_call" | custom-call | flops 3699376128 | bytes 18874368 | tf_op jit(solution)/shard_map/pallas_call | solution.py:99
  101.8 1.5 copy-done.5
  103.3 1.7 copy-done.6
  105.0 7.5 %shard_map.67 = (bf16[4,392,768]{2,1,0:T(8,128)(2,1)}, bf16[4,392,768]{2,1,0:T(8,128)(2,1)S(1)}) custom-call(s32[2]{0:T(128)S(1)} %pad_add_fusion.places.where, bf16[392,3072]{1,0:T(8,128)(2,1)S(1)} %copy-done.6, bf16[6144,512]{1,0:T(8,128)(2,1)S(1)} %get-tuple-element.18.refs_1_.refs_6_.refs_4_, ...), custom_call_target="tpu_custom_call" | custom-call | flops 3699376128 | bytes 18874368 | tf_op jit(solution)/shard_map/pallas_call | solution.py:146
  113.0 1.7 collective-permute-start.1
  114.8 1.5 shard_map.74
  118.1 2.5 %collective-permute-start.34 = (bf16[264,768]{1,0:T(8,128)(2,1)S(1)}, bf16[264,768]{1,0:T(8,128)(2,1)}, u32[]{:S(2)}, u32[]{:S(2)}) collective-permute-start(bf16[264,768]{1,0:T(8,128)(2,1)S(1)} %slice_bitcast_fusion), channel_id=1, source_target_pairs={{0,6},{1,7},{2,0},{3,1},{4,2},{5,3},{6,4},{7,5},{8,14},{9,15},{10,... | collective-permute-start | bytes 1216520 | tf_op jit(solution)/shard_map/ppermute | solution.py:49
  122.4 2.8 %copy-done.2 = bf16[512,6144]{1,0:T(8,128)(2,1)S(1)} copy-done((bf16[512,6144]{1,0:T(8,128)(2,1)S(1)}, bf16[512,6144]{1,0:T(8,128)(2,1)}, u32[]{:S(2)}) %copy-start.2) | copy-done | bytes 6291480
  125.2 3.7 %shard_map.72 = bf16[3,504,768]{2,1,0:T(8,128)(2,1)S(1)} custom-call(s32[2]{0:T(128)S(1)} %pad_add_fusion.places.where, bf16[504,512]{1,0:T(8,128)(2,1)S(1)} %get-tuple-element.28.hid, bf16[512,6144]{1,0:T(8,128)(2,1)S(1)} %copy-done.2), custom_call_target="tpu_custom_call" | custom-call | flops 1426902272 | bytes 18874368 | tf_op jit(solution)/shard_map/pallas_call | solution.py:176
  128.8 3.2 %collective-permute-done.32 = bf16[240,768]{1,0:T(8,128)(2,1)} collective-permute-done((bf16[240,768]{1,0:T(8,128)(2,1)}, bf16[240,768]{1,0:T(8,128)(2,1)}, u32[]{:S(2)}, u32[]{:S(2)}) %collective-permute-start.32) | collective-permute-done | bytes 368672 | tf_op jit(solution)/shard_map/ppermute | solution.py:49
  132.0 3.3 %fusion = (bf16[504,768]{1,0:T(8,128)(2,1)}, bf16[504,768]{1,0:T(8,128)(2,1)}) fusion(bf16[3,504,768]{2,1,0:T(8,128)(2,1)} %collective-permute-done.30, bf16[3,504,768]{2,1,0:T(8,128)(2,1)S(1)} %shard_map.72, bf16[264,768]{1,0:T(8,128)(2,1)} %collective-permute-done.34, bf16[240,768]{1,0:T(8,128)(2,1)} %collective-permute-done.32), kind=kLoop, calls=%fused_computation.4 | loop fusion | flops 4644864 | bytes 5419008 | tf_op jit(solution)/shard_map/convert_element_type | solution.py:25
  135.3 3.2 %collective-permute-start.35 = (bf16[504,768]{1,0:T(8,128)(2,1)}, bf16[504,768]{1,0:T(8,128)(2,1)}, u32[]{:S(2)}, u32[]{:S(2)}) collective-permute-start(bf16[504,768]{1,0:T(8,128)(2,1)} %get-tuple-element.35), channel_id=1, source_target_pairs={{0,6},{1,7},{2,0},{3,1},{4,2},{5,3},{6,4},{7,5},{8,14},{9,15},{10,... | collective-permute-start | bytes 2322440 | tf_op jit(solution)/shard_map/ppermute | solution.py:49
  138.5 1.5 convert_add_fusion
  140.5 3.8 %add_convert_fusion = bf16[4,392,768]{2,1,0:T(8,128)(2,1)} fusion(bf16[4,392,768]{2,1,0:T(8,128)(2,1)} %collective-permute-done.14, bf16[4,392,768]{2,1,0:T(8,128)(2,1)S(1)} %copy-done.4), kind=kLoop, calls=%fused_computation | loop fusion | flops 4816896 | bytes 7225344 | tf_op jit(solution)/shard_map/convert_element_type | solution.py:25
  144.2 10.1 %collective-permute-done.33 = bf16[504,768]{1,0:T(8,128)(2,1)S(1)} collective-permute-done((bf16[504,768]{1,0:T(8,128)(2,1)}, bf16[504,768]{1,0:T(8,128)(2,1)S(1)}, u32[]{:S(2)}, u32[]{:S(2)}) %collective-permute-start.33) | collective-permute-done | bytes 774176 | tf_op jit(solution)/shard_map/ppermute | solution.py:49
  154.3 2.5 %shard_map.75 = bf16[16,56,768]{2,1,0:T(8,128)(2,1)} custom-call(s32[16]{0:T(128)S(1)} %stack.123.homes, f32[9,56,768]{2,1,0:T(8,128)S(1)} %bitcast.62, bf16[9,56,768]{2,1,0:T(8,128)(2,1)S(1)} %bitcast.64, bf16[9,56,768]{2,1,0:T(8,128)(2,1)} %bitcast.39.second), custom_call_target="tpu_custom_call" | custom-call | tf_op jit(solution)/shard_map/pallas_call | solution.py:244
  156.8 8.2 %all-to-all-start.1 = ((bf16[16,56,768]{2,1,0:T(8,128)(2,1)}), bf16[16,56,768]{2,1,0:T(8,128)(2,1)S(1)}, u32[]{:S(2)}, u32[]{:S(2)}) async-start(bf16[16,56,768]{2,1,0:T(8,128)(2,1)} %shard_map.75), calls=%async_computation.1 | async-start | bytes 2752512 | tf_op jit(solution)/shard_map/all_to_all | solution.py:419
  165.0 1.8 fusion.28
  167.1 2.0 collective-permute-start.16
  169.1 3.3 %collective-permute-start.17 = (bf16[4,56,768]{2,1,0:T(8,128)(2,1)S(1)}, bf16[4,56,768]{2,1,0:T(8,128)(2,1)S(1)}, u32[]{:S(2)}, u32[]{:S(2)}) collective-permute-start(bf16[4,56,768]{2,1,0:T(8,128)(2,1)S(1)} %get-tuple-element.40), channel_id=1, source_target_pairs={{0,16},{8,24},{16,0},{24,8},{32,48},{40,56},{48,32},{56,40},{64,80... | collective-permute-start | bytes 1032200 | tf_op jit(solution)/shard_map/ppermute | solution.py:44
  172.4 2.7 %collective-permute-start.18 = (bf16[4,56,768]{2,1,0:T(8,128)(2,1)S(1)}, bf16[4,56,768]{2,1,0:T(8,128)(2,1)S(1)}, u32[]{:S(2)}, u32[]{:S(2)}) collective-permute-start(bf16[4,56,768]{2,1,0:T(8,128)(2,1)S(1)} %get-tuple-element.39), channel_id=1, source_target_pairs={{0,96},{8,104},{16,112},{24,120},{32,0},{40,8},{48,16},{56,24},{64... | collective-permute-start | bytes 1032200 | tf_op jit(solution)/shard_map/ppermute | solution.py:44
  175.1 14.6 %collective-permute-done.15.refs_1_ = bf16[4,56,768]{2,1,0:T(8,128)(2,1)S(1)} collective-permute-done((bf16[4,56,768]{2,1,0:T(8,128)(2,1)S(1)}, bf16[4,56,768]{2,1,0:T(8,128)(2,1)S(1)}, u32[]{:S(2)}, u32[]{:S(2)}) %collective-permute-start.15) | collective-permute-done | bytes 344096 | tf_op jit(solution)/shard_map/ppermute | solution.py:44
  189.6 3.0 %collective-permute-start.20 = (bf16[4,56,768]{2,1,0:T(8,128)(2,1)S(1)}, bf16[4,56,768]{2,1,0:T(8,128)(2,1)S(1)}, u32[]{:S(2)}, u32[]{:S(2)}) collective-permute-start(bf16[4,56,768]{2,1,0:T(8,128)(2,1)S(1)} %get-tuple-element.37), channel_id=1, source_target_pairs={{0,64},{8,72},{16,80},{24,88},{32,96},{40,104},{48,112},{56,120},{... | collective-permute-start | bytes 1032200 | tf_op jit(solution)/shard_map/ppermute | solution.py:44
  192.8 1.9 collective-permute-done.17.refs_3_
  194.7 4.8 %collective-permute-done.20.refs_6_ = bf16[4,56,768]{2,1,0:T(8,128)(2,1)S(1)} collective-permute-done((bf16[4,56,768]{2,1,0:T(8,128)(2,1)S(1)}, bf16[4,56,768]{2,1,0:T(8,128)(2,1)S(1)}, u32[]{:S(2)}, u32[]{:S(2)}) %collective-permute-start.20) | collective-permute-done | bytes 344096 | tf_op jit(solution)/shard_map/ppermute | solution.py:44
  199.5 3.0 %shard_map.68 = (f32[128,768]{1,0:T(8,128)S(1)}, bf16[3,128,768]{2,1,0:T(8,128)(2,1)S(1)}) custom-call(bf16[392,128]{1,0:T(8,128)(2,1)S(1)} %get-tuple-element.34.high, bf16[392,128]{1,0:T(8,128)(2,1)S(1)} %get-tuple-element.33.low, bf16[4,56,768]{2,1,0:T(8,128)(2,1)S(1)} %get-tuple-element.43.refs_0_, ...), custom_call_target="tpu_custom_call" | custom-call | tf_op jit(solution)/shard_map/pallas_call | solution.py:294
  202.9 2.9 %collective-permute-start.37 = (bf16[128,768]{1,0:T(8,128)(2,1)S(1)}, bf16[128,768]{1,0:T(8,128)(2,1)S(1)}, u32[]{:S(2)}, u32[]{:S(2)}) collective-permute-start(bf16[128,768]{1,0:T(8,128)(2,1)S(1)} %get-tuple-element.52), channel_id=1, source_target_pairs={{0,6},{1,7},{2,0},{3,1},{4,2},{5,3},{6,4},{7,5},{8,14},{9,15},{10,... | collective-permute-start | bytes 589832 | tf_op jit(solution)/shard_map/ppermute | solution.py:49
  206.6 4.5 %collective-permute-done.36.refs_0_ = bf16[128,768]{1,0:T(8,128)(2,1)S(1)} collective-permute-done((bf16[128,768]{1,0:T(8,128)(2,1)S(1)}, bf16[128,768]{1,0:T(8,128)(2,1)S(1)}, u32[]{:S(2)}, u32[]{:S(2)}) %collective-permute-start.36) | collective-permute-done | bytes 196640 | tf_op jit(solution)/shard_map/ppermute | solution.py:49
  211.6 1.6 collective-permute-done.38.refs_2_
  (108 shorter events, 20.9 us)
Async XLA Ops:
  0.0 112.7 %copy-start = (bf16[768,8]{0,1:T(8,128)(2,1)S(1)}, bf16[768,8]{0,1:T(8,128)(2,1)}, u32[]{:S(2)}) copy-start(bf16[768,8]{0,1:T(8,128)(2,1)} %param.7) | copy-start | bytes 36868
  0.0 18.8 %collective-permute-start.6 = (bf16[128,768]{1,0:T(8,128)(2,1)}, bf16[128,768]{1,0:T(8,128)(2,1)S(1)}, u32[]{:S(2)}, u32[]{:S(2)}) collective-permute-start(bf16[128,768]{1,0:T(8,128)(2,1)} %param.6), channel_id=1, source_target_pairs={{0,4},{1,5},{2,6},{3,7},{4,0},{5,1},{6,2},{7,3},{8,12},{9,13},{10,... | collective-permute-start | bytes 589832 | tf_op jit(solution)/shard_map/ppermute | solution.py:49
  3.2 15.6 %collective-permute-start.5 = (bf16[128,768]{1,0:T(8,128)(2,1)}, bf16[128,768]{1,0:T(8,128)(2,1)S(1)}, u32[]{:S(2)}, u32[]{:S(2)}) collective-permute-start(bf16[128,768]{1,0:T(8,128)(2,1)} %param.6), channel_id=1, source_target_pairs={{0,6},{1,7},{2,0},{3,1},{4,2},{5,3},{6,4},{7,5},{8,14},{9,15},{10,... | collective-permute-start | bytes 589832 | tf_op jit(solution)/shard_map/ppermute | solution.py:49
  4.3 14.6 %collective-permute-start.4 = (bf16[128,768]{1,0:T(8,128)(2,1)}, bf16[128,768]{1,0:T(8,128)(2,1)S(1)}, u32[]{:S(2)}, u32[]{:S(2)}) collective-permute-start(bf16[128,768]{1,0:T(8,128)(2,1)} %param.6), channel_id=1, source_target_pairs={{0,2},{1,3},{2,4},{3,5},{4,6},{5,7},{6,0},{7,1},{8,10},{9,11},{10,... | collective-permute-start | bytes 589832 | tf_op jit(solution)/shard_map/ppermute | solution.py:49
  7.5 11.4 %copy-start.7 = (bf16[128,768]{1,0:T(8,128)(2,1)S(1)}, bf16[128,768]{1,0:T(8,128)(2,1)}, u32[]{:S(2)}) copy-start(bf16[128,768]{1,0:T(8,128)(2,1)} %param.6) | copy-start | bytes 589828
  10.1 29.0 %all-to-all-start = ((bf16[16,56,768]{2,1,0:T(8,128)(2,1)}), bf16[16,56,768]{2,1,0:T(8,128)(2,1)S(1)}, u32[]{:S(2)}, u32[]{:S(2)}) async-start(bf16[16,56,768]{2,1,0:T(8,128)(2,1)} %bitcast.31), calls=%async_computation | async-start | bytes 2752512 | tf_op jit(solution)/shard_map/all_to_all | solution.py:339
  21.0 27.2 %collective-permute-start.7 = (bf16[56,3072]{1,0:T(8,128)(2,1)}, bf16[56,3072]{1,0:T(8,128)(2,1)S(1)}, u32[]{:S(2)}, u32[]{:S(2)}) collective-permute-start(bf16[56,3072]{1,0:T(8,128)(2,1)} %get-tuple-element.49), channel_id=1, source_target_pairs={{0,8},{8,16},{16,24},{24,0},{32,40},{40,48},{48,56},{56,32},{64,72... | collective-permute-start | bytes 1032200 | tf_op jit(solution)/shard_map/ppermute | solution.py:44
  22.4 25.8 %collective-permute-start.8 = (bf16[56,3072]{1,0:T(8,128)(2,1)}, bf16[56,3072]{1,0:T(8,128)(2,1)S(1)}, u32[]{:S(2)}, u32[]{:S(2)}) collective-permute-start(bf16[56,3072]{1,0:T(8,128)(2,1)} %get-tuple-element.48), channel_id=1, source_target_pairs={{0,24},{8,0},{16,8},{24,16},{32,56},{40,32},{48,40},{56,48},{64,88... | collective-permute-start | bytes 1032200 | tf_op jit(solution)/shard_map/ppermute | solution.py:44
  23.0 28.5 %collective-permute-start.9 = (bf16[56,3072]{1,0:T(8,128)(2,1)}, bf16[56,3072]{1,0:T(8,128)(2,1)S(1)}, u32[]{:S(2)}, u32[]{:S(2)}) collective-permute-start(bf16[56,3072]{1,0:T(8,128)(2,1)} %get-tuple-element.47), channel_id=1, source_target_pairs={{0,16},{8,24},{16,0},{24,8},{32,48},{40,56},{48,32},{56,40},{64,80... | collective-permute-start | bytes 1032200 | tf_op jit(solution)/shard_map/ppermute | solution.py:44
  39.7 28.2 %collective-permute-start.21 = (bf16[504,768]{1,0:T(8,128)(2,1)S(1)}, bf16[504,768]{1,0:T(8,128)(2,1)}, u32[]{:S(2)}, u32[]{:S(2)}) collective-permute-start(bf16[504,768]{1,0:T(8,128)(2,1)S(1)} %bitcast.65), channel_id=1, source_target_pairs={{0,2},{1,3},{2,4},{3,5},{4,6},{5,7},{6,0},{7,1},{8,10},{9,11},{10,... | collective-permute-start | bytes 2322440 | tf_op jit(solution)/shard_map/ppermute | solution.py:49
  40.5 27.9 %collective-permute-start.23 = (bf16[504,768]{1,0:T(8,128)(2,1)S(1)}, bf16[504,768]{1,0:T(8,128)(2,1)}, u32[]{:S(2)}, u32[]{:S(2)}) collective-permute-start(bf16[504,768]{1,0:T(8,128)(2,1)S(1)} %bitcast.66), channel_id=1, source_target_pairs={{0,6},{1,7},{2,0},{3,1},{4,2},{5,3},{6,4},{7,5},{8,14},{9,15},{10,... | collective-permute-start | bytes 2322440 | tf_op jit(solution)/shard_map/ppermute | solution.py:49
  48.2 12.4 %collective-permute-start.10 = (bf16[56,3072]{1,0:T(8,128)(2,1)}, bf16[56,3072]{1,0:T(8,128)(2,1)S(1)}, u32[]{:S(2)}, u32[]{:S(2)}) collective-permute-start(bf16[56,3072]{1,0:T(8,128)(2,1)} %get-tuple-element.46), channel_id=1, source_target_pairs={{0,32},{8,40},{16,48},{24,56},{32,64},{40,72},{48,80},{56,88},{64,... | collective-permute-start | bytes 1032200 | tf_op jit(solution)/shard_map/ppermute | solution.py:44
  48.2 18.2 %collective-permute-start.11 = (bf16[56,3072]{1,0:T(8,128)(2,1)}, bf16[56,3072]{1,0:T(8,128)(2,1)S(1)}, u32[]{:S(2)}, u32[]{:S(2)}) collective-permute-start(bf16[56,3072]{1,0:T(8,128)(2,1)} %get-tuple-element.45), channel_id=1, source_target_pairs={{0,96},{8,104},{16,112},{24,120},{32,0},{40,8},{48,16},{56,24},{64... | collective-permute-start | bytes 1032200 | tf_op jit(solution)/shard_map/ppermute | solution.py:44
  51.5 15.6 %collective-permute-start.12 = (bf16[56,3072]{1,0:T(8,128)(2,1)}, bf16[56,3072]{1,0:T(8,128)(2,1)S(1)}, u32[]{:S(2)}, u32[]{:S(2)}) collective-permute-start(bf16[56,3072]{1,0:T(8,128)(2,1)} %get-tuple-element.44), channel_id=1, source_target_pairs={{0,64},{8,72},{16,80},{24,88},{32,96},{40,104},{48,112},{56,120},{... | collective-permute-start | bytes 1032200 | tf_op jit(solution)/shard_map/ppermute | solution.py:44
  60.6 12.3 %collective-permute-start.27 = (bf16[504,768]{1,0:T(8,128)(2,1)S(1)}, bf16[504,768]{1,0:T(8,128)(2,1)S(1)}, u32[]{:S(2)}, u32[]{:S(2)}) collective-permute-start(bf16[504,768]{1,0:T(8,128)(2,1)S(1)} %bitcast.67), channel_id=1, source_target_pairs={{0,1},{1,0},{2,3},{3,2},{4,5},{5,4},{6,7},{7,6},{8,9},{9,8},{10,11... | collective-permute-start | bytes 2322440 | tf_op jit(solution)/shard_map/ppermute | solution.py:53
  67.8 34.0 %collective-permute-start.13 = (bf16[392,3072]{1,0:T(8,128)(2,1)S(1)}, bf16[392,3072]{1,0:T(8,128)(2,1)S(1)}, u32[]{:S(2)}, u32[]{:S(2)}) collective-permute-start(bf16[392,3072]{1,0:T(8,128)(2,1)S(1)} %bitcast.60), channel_id=1, source_target_pairs={{0,1},{1,0},{2,3},{3,2},{4,5},{5,4},{6,7},{7,6},{8,9},{9,8},{10,11... | collective-permute-start | bytes 7225352 | tf_op jit(solution)/shard_map/ppermute | solution.py:53
  67.9 17.4 %collective-permute-start.28 = (bf16[504,768]{1,0:T(8,128)(2,1)}, bf16[504,768]{1,0:T(8,128)(2,1)S(1)}, u32[]{:S(2)}, u32[]{:S(2)}) collective-permute-start(bf16[504,768]{1,0:T(8,128)(2,1)} %collective-permute-done.21.refs_1_), channel_id=1, source_target_pairs={{0,1},{1,0},{2,3},{3,2},{4,5},{5,4},{6,7},{7,6},{8,9},{9,8},{10,11... | collective-permute-start | bytes 2322440 | tf_op jit(solution)/shard_map/ppermute | solution.py:53
  68.4 16.9 %collective-permute-start.29 = (bf16[504,768]{1,0:T(8,128)(2,1)}, bf16[504,768]{1,0:T(8,128)(2,1)S(1)}, u32[]{:S(2)}, u32[]{:S(2)}) collective-permute-start(bf16[504,768]{1,0:T(8,128)(2,1)} %collective-permute-done.23.refs_2_), channel_id=1, source_target_pairs={{0,1},{1,0},{2,3},{3,2},{4,5},{5,4},{6,7},{7,6},{8,9},{9,8},{10,11... | collective-permute-start | bytes 2322440 | tf_op jit(solution)/shard_map/ppermute | solution.py:53
  69.5 15.3 %collective-permute-start.24 = (bf16[264,768]{1,0:T(8,128)(2,1)S(1)}, bf16[264,768]{1,0:T(8,128)(2,1)S(1)}, u32[]{:S(2)}, u32[]{:S(2)}) collective-permute-start(bf16[264,768]{1,0:T(8,128)(2,1)S(1)} %slice.131), channel_id=1, source_target_pairs={{0,6},{1,7},{2,0},{3,1},{4,2},{5,3},{6,4},{7,5},{8,14},{9,15},{10,... | collective-permute-start | bytes 1216520 | tf_op jit(solution)/shard_map/ppermute | solution.py:49
  72.9 11.9 %collective-permute-start.22 = (bf16[240,768]{1,0:T(8,128)(2,1)S(1)}, bf16[240,768]{1,0:T(8,128)(2,1)S(1)}, u32[]{:S(2)}, u32[]{:S(2)}) collective-permute-start(bf16[240,768]{1,0:T(8,128)(2,1)S(1)} %slice.130), channel_id=1, source_target_pairs={{0,2},{1,3},{2,4},{3,5},{4,6},{5,7},{6,0},{7,1},{8,10},{9,11},{10,... | collective-permute-start | bytes 1105928 | tf_op jit(solution)/shard_map/ppermute | solution.py:49
  79.4 35.4 %copy-start.1 = (bf16[512,6144]{1,0:T(8,128)(2,1)}, bf16[512,6144]{1,0:T(8,128)(2,1)S(1)}, u32[]{:S(2)}) copy-start(bf16[512,6144]{1,0:T(8,128)(2,1)S(1)} %get-tuple-element.20.refs_3_.refs_6_.down_w) | copy-start | bytes 18874372
  84.8 6.9 %collective-permute-start.25 = (bf16[240,768]{1,0:T(8,128)(2,1)S(1)}, bf16[240,768]{1,0:T(8,128)(2,1)S(1)}, u32[]{:S(2)}, u32[]{:S(2)}) collective-permute-start(bf16[240,768]{1,0:T(8,128)(2,1)S(1)} %collective-permute-done.22.refs_0_), channel_id=1, source_target_pairs={{0,1},{1,0},{2,3},{3,2},{4,5},{5,4},{6,7},{7,6},{8,9},{9,8},{10,11... | collective-permute-start | bytes 1105928 | tf_op jit(solution)/shard_map/ppermute | solution.py:53
  84.8 6.9 %collective-permute-start.26 = (bf16[264,768]{1,0:T(8,128)(2,1)S(1)}, bf16[264,768]{1,0:T(8,128)(2,1)S(1)}, u32[]{:S(2)}, u32[]{:S(2)}) collective-permute-start(bf16[264,768]{1,0:T(8,128)(2,1)S(1)} %collective-permute-done.24.refs_1_), channel_id=1, source_target_pairs={{0,1},{1,0},{2,3},{3,2},{4,5},{5,4},{6,7},{7,6},{8,9},{9,8},{10,11... | collective-permute-start | bytes 1216520 | tf_op jit(solution)/shard_map/ppermute | solution.py:53
  97.9 34.1 %collective-permute-start.30 = (bf16[3,504,768]{2,1,0:T(8,128)(2,1)}, bf16[3,504,768]{2,1,0:T(8,128)(2,1)}, u32[]{:S(2)}, u32[]{:S(2)}) collective-permute-start(bf16[3,504,768]{2,1,0:T(8,128)(2,1)} %shard_map.73), channel_id=1, source_target_pairs={{0,1},{1,0},{2,3},{3,2},{4,5},{5,4},{6,7},{7,6},{8,9},{9,8},{10,11... | collective-permute-start | bytes 6967304 | tf_op jit(solution)/shard_map/ppermute | solution.py:53
  101.3 15.0 %collective-permute-start.31 = (bf16[1,504,768]{2,1,0:T(8,128)(2,1)S(1)}, bf16[1,504,768]{2,1,0:T(8,128)(2,1)S(1)}, u32[]{:S(2)}, u32[]{:S(2)}) collective-permute-start(bf16[1,504,768]{2,1,0:T(8,128)(2,1)S(1)} %get-tuple-element.29), channel_id=1, source_target_pairs={{0,1},{1,0},{2,3},{3,2},{4,5},{5,4},{6,7},{7,6},{8,9},{9,8},{10,11... | collective-permute-start | bytes 2322440 | tf_op jit(solution)/shard_map/ppermute | solution.py:53
  105.0 7.7 %copy-start.8 = (bf16[128,768]{1,0:T(8,128)(2,1)S(1)}, bf16[128,768]{1,0:T(8,128)(2,1)}, u32[]{:S(2)}) copy-start(bf16[128,768]{1,0:T(8,128)(2,1)} %param.6) | copy-start | bytes 589828
  112.5 3.8 %copy-start.3 = (bf16[4,392,768]{2,1,0:T(8,128)(2,1)}, bf16[4,392,768]{2,1,0:T(8,128)(2,1)S(1)}, u32[]{:S(2)}) copy-start(bf16[4,392,768]{2,1,0:T(8,128)(2,1)S(1)} %get-tuple-element.23) | copy-start | bytes 7225348
  112.5 27.5 %collective-permute-start.14 = (bf16[4,392,768]{2,1,0:T(8,128)(2,1)}, bf16[4,392,768]{2,1,0:T(8,128)(2,1)}, u32[]{:S(2)}, u32[]{:S(2)}) collective-permute-start(bf16[4,392,768]{2,1,0:T(8,128)(2,1)} %get-tuple-element.24), channel_id=1, source_target_pairs={{0,1},{1,0},{2,3},{3,2},{4,5},{5,4},{6,7},{7,6},{8,9},{9,8},{10,11... | collective-permute-start | bytes 7225352 | tf_op jit(solution)/shard_map/ppermute | solution.py:53
  112.8 5.3 %collective-permute-start.2 = (f32[128,8]{0,1:T(8,128)S(1)}, f32[128,8]{0,1:T(8,128)S(1)}, u32[]{:S(2)}, u32[]{:S(2)}) collective-permute-start(f32[128,8]{0,1:T(8,128)S(1)} %fusion.30), channel_id=1, source_target_pairs={{0,4},{1,5},{2,6},{3,7},{4,0},{5,1},{6,2},{7,3},{8,12},{9,13},{10,... | collective-permute-start | bytes 12296 | tf_op jit(solution)/shard_map/ppermute | solution.py:49
  113.0 7.6 %collective-permute-start.1 = (f32[128,8]{0,1:T(8,128)S(1)}, f32[128,8]{0,1:T(8,128)S(1)}, u32[]{:S(2)}, u32[]{:S(2)}) collective-permute-start(f32[128,8]{0,1:T(8,128)S(1)} %fusion.30), channel_id=1, source_target_pairs={{0,6},{1,7},{2,0},{3,1},{4,2},{5,3},{6,4},{7,5},{8,14},{9,15},{10,... | collective-permute-start | bytes 12296 | tf_op jit(solution)/shard_map/ppermute | solution.py:49
  116.3 4.9 %collective-permute-start = (f32[128,8]{0,1:T(8,128)S(1)}, f32[128,8]{0,1:T(8,128)S(1)}, u32[]{:S(2)}, u32[]{:S(2)}) collective-permute-start(f32[128,8]{0,1:T(8,128)S(1)} %fusion.30), channel_id=1, source_target_pairs={{0,2},{1,3},{2,4},{3,5},{4,6},{5,7},{6,0},{7,1},{8,10},{9,11},{10,... | collective-permute-start | bytes 12296 | tf_op jit(solution)/shard_map/ppermute | solution.py:49
  118.1 13.9 %collective-permute-start.34 = (bf16[264,768]{1,0:T(8,128)(2,1)S(1)}, bf16[264,768]{1,0:T(8,128)(2,1)}, u32[]{:S(2)}, u32[]{:S(2)}) collective-permute-start(bf16[264,768]{1,0:T(8,128)(2,1)S(1)} %slice_bitcast_fusion), channel_id=1, source_target_pairs={{0,6},{1,7},{2,0},{3,1},{4,2},{5,3},{6,4},{7,5},{8,14},{9,15},{10,... | collective-permute-start | bytes 1216520 | tf_op jit(solution)/shard_map/ppermute | solution.py:49
  120.6 11.3 %collective-permute-start.32 = (bf16[240,768]{1,0:T(8,128)(2,1)}, bf16[240,768]{1,0:T(8,128)(2,1)}, u32[]{:S(2)}, u32[]{:S(2)}) collective-permute-start(bf16[240,768]{1,0:T(8,128)(2,1)} %slice_bitcast_fusion.1), channel_id=1, source_target_pairs={{0,2},{1,3},{2,4},{3,5},{4,6},{5,7},{6,0},{7,1},{8,10},{9,11},{10,... | collective-permute-start | bytes 1105928 | tf_op jit(solution)/shard_map/ppermute | solution.py:49
  121.2 1.2 collective-permute-start.3
  122.4 2.8 %copy-start.2 = (bf16[512,6144]{1,0:T(8,128)(2,1)S(1)}, bf16[512,6144]{1,0:T(8,128)(2,1)}, u32[]{:S(2)}) copy-start(bf16[512,6144]{1,0:T(8,128)(2,1)} %copy-done.1) | copy-start | bytes 18874372
  128.8 9.7 %copy-start.9 = (s32[128,2]{0,1:T(2,128)S(1)}, s32[128,2]{0,1:T(2,128)}, u32[]{:S(2)}) copy-start(s32[128,2]{0,1:T(2,128)} %param.8) | copy-start | bytes 3076
  135.3 19.1 %collective-permute-start.33 = (bf16[504,768]{1,0:T(8,128)(2,1)}, bf16[504,768]{1,0:T(8,128)(2,1)S(1)}, u32[]{:S(2)}, u32[]{:S(2)}) collective-permute-start(bf16[504,768]{1,0:T(8,128)(2,1)} %get-tuple-element.36), channel_id=1, source_target_pairs={{0,2},{1,3},{2,4},{3,5},{4,6},{5,7},{6,0},{7,1},{8,10},{9,11},{10,... | collective-permute-start | bytes 2322440 | tf_op jit(solution)/shard_map/ppermute | solution.py:49
  135.3 19.1 %collective-permute-start.35 = (bf16[504,768]{1,0:T(8,128)(2,1)}, bf16[504,768]{1,0:T(8,128)(2,1)}, u32[]{:S(2)}, u32[]{:S(2)}) collective-permute-start(bf16[504,768]{1,0:T(8,128)(2,1)} %get-tuple-element.35), channel_id=1, source_target_pairs={{0,6},{1,7},{2,0},{3,1},{4,2},{5,3},{6,4},{7,5},{8,14},{9,15},{10,... | collective-permute-start | bytes 2322440 | tf_op jit(solution)/shard_map/ppermute | solution.py:49
  156.8 56.4 %all-to-all-start.1 = ((bf16[16,56,768]{2,1,0:T(8,128)(2,1)}), bf16[16,56,768]{2,1,0:T(8,128)(2,1)S(1)}, u32[]{:S(2)}, u32[]{:S(2)}) async-start(bf16[16,56,768]{2,1,0:T(8,128)(2,1)} %shard_map.75), calls=%async_computation.1 | async-start | bytes 2752512 | tf_op jit(solution)/shard_map/all_to_all | solution.py:419
  166.8 22.9 %collective-permute-start.15 = (bf16[4,56,768]{2,1,0:T(8,128)(2,1)S(1)}, bf16[4,56,768]{2,1,0:T(8,128)(2,1)S(1)}, u32[]{:S(2)}, u32[]{:S(2)}) collective-permute-start(bf16[4,56,768]{2,1,0:T(8,128)(2,1)S(1)} %get-tuple-element.42), channel_id=1, source_target_pairs={{0,24},{8,0},{16,8},{24,16},{32,56},{40,32},{48,40},{56,48},{64,88... | collective-permute-start | bytes 1032200 | tf_op jit(solution)/shard_map/ppermute | solution.py:44
  167.1 25.6 %collective-permute-start.16 = (bf16[4,56,768]{2,1,0:T(8,128)(2,1)S(1)}, bf16[4,56,768]{2,1,0:T(8,128)(2,1)S(1)}, u32[]{:S(2)}, u32[]{:S(2)}) collective-permute-start(bf16[4,56,768]{2,1,0:T(8,128)(2,1)S(1)} %get-tuple-element.41), channel_id=1, source_target_pairs={{0,8},{8,16},{16,24},{24,0},{32,40},{40,48},{48,56},{56,32},{64,72... | collective-permute-start | bytes 1032200 | tf_op jit(solution)/shard_map/ppermute | solution.py:44
  169.1 25.6 %collective-permute-start.17 = (bf16[4,56,768]{2,1,0:T(8,128)(2,1)S(1)}, bf16[4,56,768]{2,1,0:T(8,128)(2,1)S(1)}, u32[]{:S(2)}, u32[]{:S(2)}) collective-permute-start(bf16[4,56,768]{2,1,0:T(8,128)(2,1)S(1)} %get-tuple-element.40), channel_id=1, source_target_pairs={{0,16},{8,24},{16,0},{24,8},{32,48},{40,56},{48,32},{56,40},{64,80... | collective-permute-start | bytes 1032200 | tf_op jit(solution)/shard_map/ppermute | solution.py:44
  172.4 22.3 %collective-permute-start.18 = (bf16[4,56,768]{2,1,0:T(8,128)(2,1)S(1)}, bf16[4,56,768]{2,1,0:T(8,128)(2,1)S(1)}, u32[]{:S(2)}, u32[]{:S(2)}) collective-permute-start(bf16[4,56,768]{2,1,0:T(8,128)(2,1)S(1)} %get-tuple-element.39), channel_id=1, source_target_pairs={{0,96},{8,104},{16,112},{24,120},{32,0},{40,8},{48,16},{56,24},{64... | collective-permute-start | bytes 1032200 | tf_op jit(solution)/shard_map/ppermute | solution.py:44
  175.1 19.6 %collective-permute-start.19 = (bf16[4,56,768]{2,1,0:T(8,128)(2,1)S(1)}, bf16[4,56,768]{2,1,0:T(8,128)(2,1)S(1)}, u32[]{:S(2)}, u32[]{:S(2)}) collective-permute-start(bf16[4,56,768]{2,1,0:T(8,128)(2,1)S(1)} %get-tuple-element.38), channel_id=1, source_target_pairs={{0,32},{8,40},{16,48},{24,56},{32,64},{40,72},{48,80},{56,88},{64,... | collective-permute-start | bytes 1032200 | tf_op jit(solution)/shard_map/ppermute | solution.py:44
  189.6 9.8 %collective-permute-start.20 = (bf16[4,56,768]{2,1,0:T(8,128)(2,1)S(1)}, bf16[4,56,768]{2,1,0:T(8,128)(2,1)S(1)}, u32[]{:S(2)}, u32[]{:S(2)}) collective-permute-start(bf16[4,56,768]{2,1,0:T(8,128)(2,1)S(1)} %get-tuple-element.37), channel_id=1, source_target_pairs={{0,64},{8,72},{16,80},{24,88},{32,96},{40,104},{48,112},{56,120},{... | collective-permute-start | bytes 1032200 | tf_op jit(solution)/shard_map/ppermute | solution.py:44
  202.5 8.6 %collective-permute-start.36 = (bf16[128,768]{1,0:T(8,128)(2,1)S(1)}, bf16[128,768]{1,0:T(8,128)(2,1)S(1)}, u32[]{:S(2)}, u32[]{:S(2)}) collective-permute-start(bf16[128,768]{1,0:T(8,128)(2,1)S(1)} %get-tuple-element.53), channel_id=1, source_target_pairs={{0,2},{1,3},{2,4},{3,5},{4,6},{5,7},{6,0},{7,1},{8,10},{9,11},{10,... | collective-permute-start | bytes 589832 | tf_op jit(solution)/shard_map/ppermute | solution.py:49
  202.9 8.7 %collective-permute-start.37 = (bf16[128,768]{1,0:T(8,128)(2,1)S(1)}, bf16[128,768]{1,0:T(8,128)(2,1)S(1)}, u32[]{:S(2)}, u32[]{:S(2)}) collective-permute-start(bf16[128,768]{1,0:T(8,128)(2,1)S(1)} %get-tuple-element.52), channel_id=1, source_target_pairs={{0,6},{1,7},{2,0},{3,1},{4,2},{5,3},{6,4},{7,5},{8,14},{9,15},{10,... | collective-permute-start | bytes 589832 | tf_op jit(solution)/shard_map/ppermute | solution.py:49
  205.8 7.4 %collective-permute-start.38 = (bf16[128,768]{1,0:T(8,128)(2,1)S(1)}, bf16[128,768]{1,0:T(8,128)(2,1)S(1)}, u32[]{:S(2)}, u32[]{:S(2)}) collective-permute-start(bf16[128,768]{1,0:T(8,128)(2,1)S(1)} %get-tuple-element.51), channel_id=1, source_target_pairs={{0,4},{1,5},{2,6},{3,7},{4,0},{5,1},{6,2},{7,3},{8,12},{9,13},{10,... | collective-permute-start | bytes 589832 | tf_op jit(solution)/shard_map/ppermute | solution.py:49
  (3 other events, 5.1 us)
